TPU v7x, 32 devices: a whole 2x2x4 slice. The times are simulated.
32 devices in a mesh: section: 8 (over z, core), sp: 4 (over y, x).
Axes of the slice: x: 2, y: 2, z: 4, core: 2. Of those that a mesh axis runs over, the one named last changes fastest.
Arguments:
- query: bfloat16 [8, 512, 8192], P('section', 'sp'), may hold values from -11 to 11
- keyval: bfloat16 [8, 512, 2048], P('section', 'sp'), may hold values from -11 to 11
- cache: bfloat16 [8, 8, 256, 256], P('section', 'sp'), may hold values from -4 to 4, as said below
- offsets: int32 [8], P('section'), may hold values from 0 to 8191
- lengths: int32 [8], P('section'), may hold values from 1 to 256
Outputs:
- forwarded: bfloat16 [8, 512, 8192], P('section', 'sp')
Inputs may be any that keep to these rules, and one draw needn't show every extreme that they name: `cache`: slot k holds key-value head k * 1; slots that hold the same head are equal.
All inputs are finite; a program needn't handle non-finite values.
Results may differ from a plain program's by a relative error of at most 0.0096.
Values may be sent and summed in bfloat16 or wider, within the bound.
No kernel may reach another device: no remote copies, remote signals or barrier semaphores. Data moves between devices by JAX's collectives and lax.ppermute only.
A program may use at most 64 MiB of HBM per device.

v0:
```python
import math

import jax
import jax.numpy as jnp
from jax import lax
from jax.sharding import PartitionSpec as P

QUERY_HEADS = 64
KEY_VALUE_HEADS = 8
HEAD_SIZE = 128


ROPE_BASE = 500000.0


def passed_along(value, axis, steps):
    count = lax.axis_size(axis)
    pairs = [(source, (source + steps) % count) for source in range(count)]
    return lax.ppermute(value, axis, pairs)


def rotation_tables(positions, head_width):
    half_width = head_width // 2
    exponent = jnp.arange(half_width, dtype=jnp.float32) * (-2.0 / head_width)
    frequency = jnp.power(jnp.float32(ROPE_BASE), exponent)
    angle = positions.astype(jnp.float32)[:, None] * frequency[None, :]
    return (jnp.cos(angle), jnp.sin(angle))


def rotate_pair(value_entries, cosine, sine):
    half_width = value_entries.shape[-1] // 2
    first = value_entries[..., :half_width].astype(jnp.float32)
    second = value_entries[..., half_width:].astype(jnp.float32)
    cos_wide = cosine[:, None, :]
    sin_wide = sine[:, None, :]
    return jnp.concatenate(
        [first * cos_wide - second * sin_wide, second * cos_wide + first * sin_wide], axis=-1
    )


def attend_head(query_rows, key_rows, value_rows, cache_keys, cache_values, length, block_rows):
    scale = 1.0 / math.sqrt(query_rows.shape[-1])
    contract = (((1,), (1,)), ((), ()))
    cache_live = jnp.arange(cache_keys.shape[0], dtype=jnp.int32) < length
    results = []
    for block_index in range(query_rows.shape[0] // block_rows):
        first_row = block_index * block_rows
        key_reach = first_row + block_rows
        block_queries = query_rows[first_row:key_reach]
        cache_scores = (
            lax.dot_general(block_queries, cache_keys, contract, preferred_element_type=jnp.float32)
            * scale
        )
        own_scores = (
            lax.dot_general(
                block_queries, key_rows[:key_reach], contract, preferred_element_type=jnp.float32
            )
            * scale
        )
        cache_scores = jnp.where(cache_live[None, :], cache_scores, -jnp.inf)
        row_place = first_row + jnp.arange(block_rows, dtype=jnp.int32)
        causal = jnp.arange(key_reach, dtype=jnp.int32)[None, :] <= row_place[:, None]
        own_scores = jnp.where(causal, own_scores, -jnp.inf)
        row_top = jnp.maximum(jnp.max(cache_scores, axis=1), jnp.max(own_scores, axis=1))
        cache_weights = jnp.exp(cache_scores - row_top[:, None])
        own_weights = jnp.exp(own_scores - row_top[:, None])
        row_total = jnp.sum(cache_weights, axis=1) + jnp.sum(own_weights, axis=1)
        numerator = jnp.dot(
            cache_weights.astype(jnp.bfloat16), cache_values, preferred_element_type=jnp.float32
        )
        numerator = numerator + jnp.dot(
            own_weights.astype(jnp.bfloat16),
            value_rows[:key_reach],
            preferred_element_type=jnp.float32,
        )
        results.append((numerator / row_total[:, None]).astype(jnp.bfloat16))
    return jnp.concatenate(results, axis=0)


def on_device(query, keyval, cache, offsets, lengths):
    token_row_block = query.shape[1]
    group_total = lax.axis_size("sp")
    local_slots = cache.shape[1]
    head_copies = local_slots * group_total // KEY_VALUE_HEADS
    local_queries = query[0].reshape(token_row_block, QUERY_HEADS, HEAD_SIZE)
    head_queries = lax.all_to_all(local_queries, "sp", split_axis=1, concat_axis=0, tiled=True)
    span_rows = head_queries.shape[0]
    heads_here = head_queries.shape[1]
    local_head_pairs = keyval[0].reshape(token_row_block, KEY_VALUE_HEADS, 2 * HEAD_SIZE)
    broadened = jnp.repeat(local_head_pairs, head_copies, axis=1)
    head_pairs = lax.all_to_all(broadened, "sp", split_axis=1, concat_axis=0, tiled=True)
    positions = offsets[0] + jnp.arange(span_rows, dtype=jnp.int32)
    cosine, sine = rotation_tables(positions, HEAD_SIZE)
    rotated_keys = rotate_pair(head_pairs[..., :HEAD_SIZE], cosine, sine).astype(jnp.bfloat16)
    plain_values = head_pairs[..., HEAD_SIZE:]
    section_cache = cache[0]
    length = lengths[0]
    per_slot = heads_here // local_slots
    block_rows = min(512, span_rows)

    def head_step(head_index, finished):
        slot_index = head_index // per_slot
        picked = lax.dynamic_slice_in_dim(head_queries, head_index, 1, 1)
        rotated = rotate_pair(picked, cosine, sine)[:, 0].astype(jnp.bfloat16)
        slot_keys = lax.dynamic_index_in_dim(rotated_keys, slot_index, 1, False)
        slot_values = lax.dynamic_index_in_dim(plain_values, slot_index, 1, False)
        slot_cache = lax.dynamic_index_in_dim(section_cache, slot_index, 0, False)
        result = attend_head(
            rotated,
            slot_keys,
            slot_values,
            slot_cache[:, :HEAD_SIZE],
            slot_cache[:, HEAD_SIZE:],
            length,
            block_rows,
        )
        return lax.dynamic_update_slice_in_dim(finished, result[:, None, :], head_index, 1)

    finished = lax.fori_loop(
        0, heads_here, head_step, jnp.zeros((span_rows, heads_here, HEAD_SIZE), jnp.bfloat16)
    )
    passed = passed_along(finished, "section", 1)
    moved = lax.all_to_all(passed, "sp", split_axis=0, concat_axis=1, tiled=True).reshape(
        token_row_block, QUERY_HEADS * HEAD_SIZE
    )
    return moved.reshape(1, token_row_block, QUERY_HEADS * HEAD_SIZE)


def solution(mesh):
    return jax.shard_map(
        on_device,
        mesh=mesh,
        in_specs=(
            P("section", "sp", None),
            P("section", "sp", None),
            P("section", "sp", None, None),
            P("section"),
            P("section"),
        ),
        out_specs=P("section", "sp", None),
        check_vma=False,
    )
```

profile of v0, /device:TPU:0, one launch (start us, length us, event | category | flops | bytes accessed | tf_op | source)
XLA Modules:
  0.0 162.3 jit_solution(7472972265899435475)
XLA Ops:
  0.0 2.0 %copy.31 = bf16[1,128,2048]{1,2,0:T(8,128)(2,1)} copy(bf16[1,128,2048]{2,1,0:T(8,128)(2,1)} %param.8) | data formatting | bytes 1048576 | tf_op args[1]
  2.0 5.2 %all-to-all-start.1 = ((bf16[128,8,256]{0,2,1:T(8,128)(2,1)}), bf16[128,8,256]{0,2,1:T(8,128)(2,1)S(1)}, u32[]{:S(2)}, u32[]{:S(2)}) async-start(bf16[128,8,256]{0,2,1:T(8,128)(2,1)} %bitcast.7), calls=%async_computation.1 | async-start | bytes 1048576 | tf_op jit(solution)/shard_map/all_to_all | solution.py:91
  7.2 3.2 %copy.27 = bf16[1,128,8192]{1,2,0:T(8,128)(2,1)S(1)} copy(bf16[1,128,8192]{2,1,0:T(8,128)(2,1)} %param.7) | data formatting | bytes 4194304 | tf_op args[0]
  10.5 2.9 %copy.28 = bf16[128,64,128]{2,0,1:T(8,128)(2,1)} copy(bf16[128,64,128]{0,2,1:T(8,128)(2,1)S(1)} %bitcast.73) | data formatting | bytes 4194304 | tf_op jit(solution)/shard_map/reshape;squeeze | solution.py:85
  13.4 1.9 %all-to-all-done.1 = bf16[128,8,256]{0,2,1:T(8,128)(2,1)S(1)} async-done(((bf16[128,8,256]{0,2,1:T(8,128)(2,1)}), bf16[128,8,256]{0,2,1:T(8,128)(2,1)S(1)}, u32[]{:S(2)}, u32[]{:S(2)}) %all-to-all-start.1) | async-done | bytes 524320 | tf_op jit(solution)/shard_map/all_to_all | solution.py:91
  15.2 3.6 %all-to-all-start = ((bf16[128,64,128]{2,0,1:T(8,128)(2,1)}), bf16[128,64,128]{2,0,1:T(8,128)(2,1)S(1)}, u32[]{:S(2)}, u32[]{:S(2)}) async-start(bf16[128,64,128]{2,0,1:T(8,128)(2,1)} %copy.28), calls=%async_computation | async-start | bytes 4194304 | tf_op jit(solution)/shard_map/all_to_all | solution.py:86
  19.5 1.8 %multiply_cosine_fusion.1 = (f32[512,64]{1,0:T(8,128)S(1)}, f32[512,64]{1,0:T(8,128)}) fusion(f32[64]{0:T(128)S(1)} %multiply_power_fusion, f32[512]{0:T(512)S(1)} %add_convert_fusion), kind=kLoop, calls=%fused_computation.60 | loop fusion | flops 32768 | bytes 264448 | tf_op jit(solution)/shard_map/cos | solution.py:27
  21.5 0.8 slice.67
  22.3 1.2 fusion.41
  23.6 19.2 %all-to-all-done = bf16[128,64,128]{2,0,1:T(8,128)(2,1)S(1)} async-done(((bf16[128,64,128]{2,0,1:T(8,128)(2,1)}), bf16[128,64,128]{2,0,1:T(8,128)(2,1)S(1)}, u32[]{:S(2)}, u32[]{:S(2)}) %all-to-all-start) | async-done | bytes 2097184 | tf_op jit(solution)/shard_map/all_to_all | solution.py:86
  42.9 2.7 %copy.30 = bf16[4,128,16,128]{3,2,1,0:T(8,128)(2,1)} copy(bf16[4,128,16,128]{3,1,2,0:T(8,128)(2,1)S(1)} %bitcast.70) | data formatting | bytes 4194304 | tf_op jit(solution)/shard_map/all_to_all | solution.py:86
  45.6 3.1 %copy.34 = bf16[512,16,128]{0,2,1:T(8,128)(2,1)S(1)} copy(bf16[512,16,128]{2,1,0:T(8,128)(2,1)} %bitcast.71) | data formatting | bytes 4194304
  48.7 54.7 %while.17 = (s32[]{:T(128)}, bf16[512,16,128]{2,0,1:T(8,128)(2,1)}, s32[]{:T(128)}, bf16[512,16,128]{0,2,1:T(8,128)(2,1)S(1)}, bf16[2,256,256]{2,1,0:T(8,128)(2,...) while((s32[]{:T(128)}, bf16[512,16,128]{2,0,1:T(8,128)(2,1)}, ...), condition=%wide.region_5.6_spmd.clone.clone, body=%wide.region_0.5_spmd.clone.clone.sunk | while | flops 205421840 | bytes 6588201 | solution.py:119
  48.7 0.6 fusion.61
  49.6 0.7 iota_compare_fusion.3
  51.1 1.0 fusion.67
  52.1 0.6 fusion.61
  53.0 0.7 iota_compare_fusion.3
  54.5 1.0 fusion.67
  55.5 0.6 fusion.61
  56.4 0.7 iota_compare_fusion.3
  57.9 1.0 fusion.67
  59.0 0.6 fusion.61
  59.9 0.7 iota_compare_fusion.3
  61.3 1.0 fusion.67
  62.4 0.6 fusion.61
  63.3 0.7 iota_compare_fusion.3
  64.8 1.0 fusion.67
  65.8 0.6 fusion.61
  66.7 0.7 iota_compare_fusion.3
  68.2 1.0 fusion.67
  69.2 0.6 fusion.61
  70.1 0.7 iota_compare_fusion.3
  71.6 1.0 fusion.67
  72.6 0.6 fusion.61
  73.5 0.7 iota_compare_fusion.3
  75.0 1.0 fusion.67
  76.0 0.6 fusion.61
  76.9 0.7 iota_compare_fusion.3
  78.4 1.0 fusion.67
  79.5 0.6 fusion.61
  80.4 0.7 iota_compare_fusion.3
  81.9 1.0 fusion.67
  82.9 0.6 fusion.61
  83.8 0.7 iota_compare_fusion.3
  85.3 1.0 fusion.67
  86.3 0.6 fusion.61
  87.2 0.7 iota_compare_fusion.3
  88.7 1.0 fusion.67
  89.7 0.6 fusion.61
  90.6 0.7 iota_compare_fusion.3
  92.1 1.0 fusion.67
  93.1 0.6 fusion.61
  94.0 0.7 iota_compare_fusion.3
  95.5 1.0 fusion.67
  97.5 0.7 iota_compare_fusion.3
  99.0 1.0 fusion.67
  100.9 0.7 iota_compare_fusion.3
  102.4 1.0 fusion.67
  103.4 2.9 %copy.35 = bf16[512,16,128]{2,1,0:T(8,128)(2,1)S(1)} copy(bf16[512,16,128]{2,0,1:T(8,128)(2,1)} %get-tuple-element.226) | data formatting | bytes 4194304 | tf_op jit(solution)/shard_map/while | solution.py:119
  106.4 27.2 %collective-permute-done = bf16[512,16,128]{2,1,0:T(8,128)(2,1)S(1)} collective-permute-done((bf16[512,16,128]{2,1,0:T(8,128)(2,1)S(1)}, bf16[512,16,128]{2,1,0:T(8,128)(2,1)S(1)}, u32[]{:S(2)}, u32[]{:S(2)}) %collective-permute-start) | collective-permute-done | bytes 2097184 | tf_op jit(solution)/shard_map/ppermute | solution.py:19
  133.7 25.7 %all_to_all.51 = bf16[512,16,128]{2,1,0:T(8,128)(2,1)S(1)} all-to-all(bf16[512,16,128]{2,1,0:T(8,128)(2,1)S(1)} %collective-permute-done), channel_id=1, replica_groups=mesh['section'=8,'sp'=4] {'sp'}, dimensions={0} | all-to-all | bytes 4194304 | tf_op jit(solution)/shard_map/all_to_all | solution.py:123
  159.4 0.6 copy.36
  160.0 2.3 %reshape_reshape.3 = bf16[1,128,8192]{2,1,0:T(8,128)(2,1)} reshape(bf16[128,4,16,128]{3,2,1,0:T(8,128)(2,1)S(1)} %copy.36) | data formatting | bytes 4194304 | tf_op jit(solution)/shard_map/reshape;reshape | solution.py:126
  (140 shorter events, 19.6 us)
Async XLA Ops:
  2.0 13.2 %all-to-all-start.1 = ((bf16[128,8,256]{0,2,1:T(8,128)(2,1)}), bf16[128,8,256]{0,2,1:T(8,128)(2,1)S(1)}, u32[]{:S(2)}, u32[]{:S(2)}) async-start(bf16[128,8,256]{0,2,1:T(8,128)(2,1)} %bitcast.7), calls=%async_computation.1 | async-start | bytes 1048576 | tf_op jit(solution)/shard_map/all_to_all | solution.py:91
  15.2 27.6 %all-to-all-start = ((bf16[128,64,128]{2,0,1:T(8,128)(2,1)}), bf16[128,64,128]{2,0,1:T(8,128)(2,1)S(1)}, u32[]{:S(2)}, u32[]{:S(2)}) async-start(bf16[128,64,128]{2,0,1:T(8,128)(2,1)} %copy.28), calls=%async_computation | async-start | bytes 4194304 | tf_op jit(solution)/shard_map/all_to_all | solution.py:86
  45.6 3.1 %copy-start = (bf16[1,2,256,256]{3,2,1,0:T(8,128)(2,1)S(1)}, bf16[1,2,256,256]{3,2,1,0:T(8,128)(2,1)}, u32[]{:S(2)}) copy-start(bf16[1,2,256,256]{3,2,1,0:T(8,128)(2,1)} %param.9) | copy-start | bytes 786436
  45.6 3.1 %copy-start.1 = (bf16[512,2,128]{2,0,1:T(8,128)(2,1)S(1)}, bf16[512,2,128]{2,0,1:T(8,128)(2,1)}, u32[]{:S(2)}) copy-start(bf16[512,2,128]{2,0,1:T(8,128)(2,1)} %slice.67) | copy-start | bytes 786436
  106.3 27.3 %collective-permute-start = (bf16[512,16,128]{2,1,0:T(8,128)(2,1)S(1)}, bf16[512,16,128]{2,1,0:T(8,128)(2,1)S(1)}, u32[]{:S(2)}, u32[]{:S(2)}) collective-permute-start(bf16[512,16,128]{2,1,0:T(8,128)(2,1)S(1)} %copy.35), channel_id=1, source_target_pairs={{0,4},{4,8},{8,12},{12,16},{16,20},{20,24},{24,28},{28,0},{1,5},{5... | collective-permute-start | bytes 6291464 | tf_op jit(solution)/shard_map/ppermute | solution.py:19
where the time goes:
time: 163 us; the launch traced here: 162 us
  waiting for transfers between devices  48.4 us (30%)
  matrix products  29.1 us (18%)
  other arithmetic  27.8 us (17%)
  blocking collectives  25.7 us (16%)
  local copies, waits for them, and re-layouts  21 us (13%)
  starting transfers between devices  8.86 us (5%)
    ppermute x1, waiting for transfers between devices, passed_along(): return lax.ppermute(value, axis, pairs)  27.2 us
    all_to_all x1, blocking collectives, on_device(): lax.all_to_all(passed, 'sp', split_axis=0, concat_axis=1, tiled=True)  25.7 us
    all_to_all x1, waiting for transfers between devices, on_device(): lax.all_to_all(local_queries, 'sp', split_axis=1, concat_axis=0, tiled=True)  19.2 us
    dot_general x16, matrix products, attend_head(): jnp.dot(own_weights.astype(jnp.bfloat16), value_rows[:key_reach], preferr...  16.4 us
    lt x16, other arithmetic, attend_head(): cache_live = jnp.arange(cache_keys.shape[0], dtype=jnp.int32) < length  10.4 us
    another operation x17, other arithmetic  10.3 us
    unnamed x7, local copies, waits for them, and re-layouts  8.31 us
    all_to_all x1, starting transfers between devices, on_device(): lax.all_to_all(broadened, 'sp', split_axis=1, concat_axis=0, tiled=True)  5.19 us
  transfers between devices with their start and end apart: 3, of which 3 were waited for; matrix products, arithmetic and copies ran while one was open for 6% of the time, Pallas kernels for 0%

commit v1 on v0

--- a/solution.py
+++ b/solution.py
@@ -3,20 +3,39 @@
 import jax
 import jax.numpy as jnp
 from jax import lax
+from jax.experimental import pallas as pl
+from jax.experimental.pallas import tpu as pltpu
 from jax.sharding import PartitionSpec as P
+
 
 QUERY_HEADS = 64
 KEY_VALUE_HEADS = 8
 HEAD_SIZE = 128
+GROUP = QUERY_HEADS // KEY_VALUE_HEADS
 
 
 ROPE_BASE = 500000.0
-
-
-def passed_along(value, axis, steps):
-    count = lax.axis_size(axis)
-    pairs = [(source, (source + steps) % count) for source in range(count)]
-    return lax.ppermute(value, axis, pairs)
+MASKED = -1e30
+FACTOR = math.log2(math.e) / math.sqrt(HEAD_SIZE)
+SPECS = (
+    P("section", "sp", None),
+    P("section", "sp", None),
+    P("section", "sp", None, None),
+    P("section"),
+    P("section"),
+)
+VMEM = pl.BlockSpec(memory_space=pltpu.VMEM)
+LIMIT = pltpu.CompilerParams(vmem_limit_bytes=20 * 2**20)
+
+
+def section_shift(value):
+    count = lax.axis_size("section")
+    return lax.ppermute(value, "section", [(i, (i + 1) % count) for i in range(count)])
+
+
+def partner_swap(value, bits):
+    count = lax.axis_size("sp")
+    return lax.ppermute(value, "sp", [(i, i ^ bits) for i in range(count)])
 
 
 def rotation_tables(positions, head_width):
@@ -27,7 +46,206 @@
     return (jnp.cos(angle), jnp.sin(angle))
 
 
-def rotate_pair(value_entries, cosine, sine):
+def rotated(value, cosine, sine):
+    wide = value.astype(jnp.float32)
+    turned = pltpu.roll(wide, HEAD_SIZE // 2, 1)
+    return (wide * cosine + turned * sine).astype(jnp.bfloat16)
+
+
+def pack_kernel(keyval, cache, cosine, sine, length, *packs):
+    rows = keyval.shape[0]
+    cos_here, sin_here = cosine[...], sine[...]
+    positions = cache.shape[1]
+    live = length[0].astype(jnp.float32)
+    for chunk, pack in enumerate(packs):
+        heads = KEY_VALUE_HEADS // len(packs)
+        for index in range(heads):
+            head = index * len(packs) + chunk
+            start = index * rows + (positions if index >= heads // 2 else 0)
+            column = head * 2 * HEAD_SIZE
+            pack[start : start + rows, :HEAD_SIZE] = rotated(
+                keyval[:, column : column + HEAD_SIZE], cos_here, sin_here
+            )
+            pack[start : start + rows, HEAD_SIZE:] = keyval[
+                :, column + HEAD_SIZE : column + 2 * HEAD_SIZE
+            ]
+        middle = heads // 2 * rows
+        pack[middle : middle + positions, :] = cache[chunk]
+        last = heads * rows + positions
+        pack[last:, :] = jnp.full((pack.shape[0] - last, pack.shape[1]), live, jnp.float32).astype(
+            jnp.bfloat16
+        )
+
+
+def turn_kernel(query, cosine, sine, *turned):
+    rows = query.shape[0]
+    cos_here, sin_here = cosine[...], sine[...]
+    for head in range(QUERY_HEADS):
+        pair = head // GROUP
+        chunk, index = pair % len(turned), pair // len(turned)
+        start = (index * GROUP + head % GROUP) * rows
+        turned[chunk][start : start + rows, :] = rotated(
+            query[:, head * HEAD_SIZE : (head + 1) * HEAD_SIZE], cos_here, sin_here
+        )
+
+
+STEP_HEADS = GROUP
+
+
+def dot_scores(picked, keys):
+    return lax.dot_general(
+        picked, keys, (((1,), (1,)), ((), ())), preferred_element_type=jnp.float32
+    )
+
+
+def weighted(weights, values):
+    values = jnp.concatenate([values, jnp.ones_like(values)], axis=1)
+    return jnp.dot(weights, values, preferred_element_type=jnp.float32)
+
+
+def live_mask(own, positions):
+    last = own.shape[0] - 16
+    length = own[last : last + 1, :].astype(jnp.float32)
+    place = lax.broadcasted_iota(jnp.int32, (1, positions), 1).astype(jnp.float32)
+    return place < length[:, :positions]
+
+
+def near_kernel(query, own, beside, above, top_ref, sums_ref):
+    me = lax.axis_index("sp")
+    total = query.shape[0]
+    rows = 128
+    heads = total // (GROUP * rows)
+    positions = own.shape[0] - 16 - heads * rows
+    middle = heads // 2 * rows
+    blocks = (own, beside, above)
+    live = live_mask(own, positions)
+    step_rows = STEP_HEADS * rows
+    causal = lax.broadcasted_iota(jnp.int32, (rows, rows), 1) <= lax.broadcasted_iota(
+        jnp.int32, (rows, rows), 0
+    )
+    causal = jnp.concatenate([causal] * STEP_HEADS, axis=0)
+    for offset in range(len(blocks) + 1):
+        head = me ^ offset
+        start = pl.multiple_of(head * rows + jnp.where(head >= heads // 2, positions, 0), rows)
+        stored = [block[pl.ds(start, rows), :] for block in blocks]
+        if offset < len(blocks):
+            stored.append(blocks[offset][middle : middle + positions, :])
+        keys = jnp.concatenate([part[:, :HEAD_SIZE] for part in stored], axis=0)
+        values = jnp.concatenate([part[:, HEAD_SIZE:] for part in stored], axis=0)
+        base = pl.multiple_of(head * (GROUP * rows), rows)
+        for step in range(GROUP // STEP_HEADS):
+            place = pl.ds(base + step * step_rows, step_rows)
+            scores = dot_scores(query[place, :], keys)
+            parts = [jnp.where(causal, scores[:, :rows], MASKED)]
+            for other in range(1, len(blocks)):
+                piece = scores[:, other * rows : (other + 1) * rows]
+                parts.append(jnp.where((me ^ other) < me, piece, MASKED))
+            if offset < len(blocks):
+                parts.append(jnp.where(live, scores[:, len(blocks) * rows :], MASKED))
+            scores = jnp.concatenate(parts, axis=1)
+            top = jnp.max(scores, axis=1, keepdims=True)
+            weights = jnp.exp2((scores - top) * FACTOR).astype(jnp.bfloat16)
+            sums_ref[place, :] = weighted(weights, values)
+            top_ref[place, :] = jnp.broadcast_to(top, (step_rows, HEAD_SIZE))
+
+
+def far_kernel(query, own, first_half, second_half, top_ref, sums_ref, *rest):
+    passed, out, across = rest if len(rest) == 3 else (None, *rest)
+    me = lax.axis_index("sp")
+    rows = out.shape[0]
+    heads = query.shape[0] // (GROUP * rows)
+    half = first_half.shape[0]
+    positions = 2 * half - heads * rows
+    middle = heads // 2 * rows
+    width = GROUP * HEAD_SIZE
+    across[:half, :] = first_half[...]
+    across[half:, :] = second_half[...]
+    live = live_mask(own, positions)
+    step_rows = STEP_HEADS * rows
+    far = heads - 1
+    if passed is not None:
+        for index in range(heads):
+            out[:, 2 * index * width : (2 * index + 1) * width] = passed[
+                :, index * width : (index + 1) * width
+            ]
+    for offset in range(heads):
+        head = me ^ offset
+        start = pl.multiple_of(head * rows + jnp.where(head >= heads // 2, positions, 0), rows)
+        stored = [across[pl.ds(start, rows), :]]
+        if offset == far:
+            stored.append(across[middle : middle + positions, :])
+        keys = jnp.concatenate([part[:, :HEAD_SIZE] for part in stored], axis=0)
+        values = jnp.concatenate([part[:, HEAD_SIZE:] for part in stored], axis=0)
+        base = pl.multiple_of(head * (GROUP * rows), rows)
+        for step in range(GROUP // STEP_HEADS):
+            place = pl.ds(base + step * step_rows, step_rows)
+            scores = dot_scores(query[place, :], keys)
+            parts = [jnp.where((me ^ far) < me, scores[:, :rows], MASKED)]
+            if offset == far:
+                parts.append(jnp.where(live, scores[:, rows:], MASKED))
+            scores = jnp.concatenate(parts, axis=1)
+            before = top_ref[place, :]
+            top = jnp.maximum(jnp.max(scores, axis=1, keepdims=True), before)
+            kept = jnp.exp2((before - top) * FACTOR)
+            weights = jnp.exp2(
+                (scores - jnp.concatenate([top] * len(parts[:1] + parts[1:] * 2), axis=1)) * FACTOR
+            ).astype(jnp.bfloat16)
+            sums = weighted(weights, values) + sums_ref[place, :] * jnp.concatenate(
+                [kept, kept], axis=1
+            )
+            result = (sums[:, :HEAD_SIZE] / sums[:, HEAD_SIZE:]).astype(jnp.bfloat16)
+            for part in range(STEP_HEADS):
+                lane = (step * STEP_HEADS + part) * HEAD_SIZE
+                if passed is None:
+                    column = head * width + lane
+                else:
+                    column = (2 * head + 1) * width + lane
+                out[:, pl.ds(pl.multiple_of(column, HEAD_SIZE), HEAD_SIZE)] = result[
+                    part * rows : (part + 1) * rows
+                ]
+
+
+def near(turned, own, beside, above):
+    work = turned.shape[0] * 576
+    return pl.pallas_call(
+        near_kernel,
+        out_shape=[
+            jax.ShapeDtypeStruct((turned.shape[0], HEAD_SIZE), jnp.float32),
+            jax.ShapeDtypeStruct((turned.shape[0], 2 * HEAD_SIZE), jnp.float32),
+        ],
+        in_specs=[VMEM] * 4,
+        out_specs=[VMEM] * 2,
+        compiler_params=LIMIT,
+        cost_estimate=pl.CostEstimate(
+            flops=12 * work * HEAD_SIZE, bytes_accessed=4 * turned.size, transcendentals=work
+        ),
+    )(turned, own, beside, above)
+
+
+def far(turned, own, first_half, second_half, state, rows, passed=None):
+    work = turned.shape[0] * 192
+    width = turned.shape[0] // rows * HEAD_SIZE
+    extra = [] if passed is None else [passed]
+    return pl.pallas_call(
+        far_kernel,
+        out_shape=jax.ShapeDtypeStruct((rows, width * (1 + len(extra))), jnp.bfloat16),
+        in_specs=[VMEM] * (6 + len(extra)),
+        out_specs=VMEM,
+        scratch_shapes=[pltpu.VMEM((2 * first_half.shape[0], own.shape[1]), jnp.bfloat16)],
+        compiler_params=LIMIT,
+        cost_estimate=pl.CostEstimate(
+            flops=12 * work * HEAD_SIZE, bytes_accessed=4 * turned.size, transcendentals=work
+        ),
+    )(turned, own, first_half, second_half, *state, *extra)
+
+
+def passed_along(value, axis, steps):
+    count = lax.axis_size(axis)
+    pairs = [(source, (source + steps) % count) for source in range(count)]
+    return lax.ppermute(value, axis, pairs)
+
+
+def turned_pair(value_entries, cosine, sine):
     half_width = value_entries.shape[-1] // 2
     first = value_entries[..., :half_width].astype(jnp.float32)
     second = value_entries[..., half_width:].astype(jnp.float32)
@@ -77,7 +295,7 @@
     return jnp.concatenate(results, axis=0)
 
 
-def on_device(query, keyval, cache, offsets, lengths):
+def head_exchange(query, keyval, cache, offsets, lengths):
     token_row_block = query.shape[1]
     group_total = lax.axis_size("sp")
     local_slots = cache.shape[1]
@@ -91,7 +309,7 @@
     head_pairs = lax.all_to_all(broadened, "sp", split_axis=1, concat_axis=0, tiled=True)
     positions = offsets[0] + jnp.arange(span_rows, dtype=jnp.int32)
     cosine, sine = rotation_tables(positions, HEAD_SIZE)
-    rotated_keys = rotate_pair(head_pairs[..., :HEAD_SIZE], cosine, sine).astype(jnp.bfloat16)
+    rotated_keys = turned_pair(head_pairs[..., :HEAD_SIZE], cosine, sine).astype(jnp.bfloat16)
     plain_values = head_pairs[..., HEAD_SIZE:]
     section_cache = cache[0]
     length = lengths[0]
@@ -101,7 +319,7 @@
     def head_step(head_index, finished):
         slot_index = head_index // per_slot
         picked = lax.dynamic_slice_in_dim(head_queries, head_index, 1, 1)
-        rotated = rotate_pair(picked, cosine, sine)[:, 0].astype(jnp.bfloat16)
+        rotated = turned_pair(picked, cosine, sine)[:, 0].astype(jnp.bfloat16)
         slot_keys = lax.dynamic_index_in_dim(rotated_keys, slot_index, 1, False)
         slot_values = lax.dynamic_index_in_dim(plain_values, slot_index, 1, False)
         slot_cache = lax.dynamic_index_in_dim(section_cache, slot_index, 0, False)
@@ -126,17 +344,62 @@
     return moved.reshape(1, token_row_block, QUERY_HEADS * HEAD_SIZE)
 
 
+def on_device(query, keyval, cache, offsets, lengths):
+    rows = query.shape[1]
+    chunks = cache.shape[1]
+    heads = KEY_VALUE_HEADS // chunks
+    positions = offsets[0] + lax.axis_index("sp") * rows + jnp.arange(rows, dtype=jnp.int32)
+    cosine, sine = rotation_tables(positions, HEAD_SIZE)
+    cosine = jnp.concatenate([cosine, cosine], axis=1)
+    sine = jnp.concatenate([-sine, sine], axis=1)
+    pack_rows = heads * rows + cache.shape[2] + 16
+    half = (pack_rows - 16) // 2
+    here, ahead = pl.pallas_call(
+        pack_kernel,
+        out_shape=[jax.ShapeDtypeStruct((pack_rows, 2 * HEAD_SIZE), jnp.bfloat16)] * chunks,
+        in_specs=[VMEM] * 4 + [pl.BlockSpec(memory_space=pltpu.SMEM)],
+        out_specs=[VMEM] * chunks,
+        compiler_params=LIMIT,
+        cost_estimate=pl.CostEstimate(flops=2**30, bytes_accessed=2**21, transcendentals=0),
+    )(keyval[0], cache[0], cosine, sine, lengths)
+    turned_here, turned_ahead = pl.pallas_call(
+        turn_kernel,
+        out_shape=[
+            jax.ShapeDtypeStruct((query.size // (HEAD_SIZE * chunks), HEAD_SIZE), jnp.bfloat16)
+        ]
+        * chunks,
+        in_specs=[VMEM] * 3,
+        out_specs=[VMEM] * chunks,
+        compiler_params=LIMIT,
+        cost_estimate=pl.CostEstimate(flops=2**30, bytes_accessed=2**23, transcendentals=0),
+    )(query[0], cosine, sine)
+    beside = partner_swap(here, 1)
+    above = partner_swap(here, 2)
+    moved_pack = section_shift(ahead)
+    moved_query = section_shift(turned_ahead)
+    first_half = partner_swap(beside[:half], 2)
+    second_half = partner_swap(above[half : 2 * half], 1)
+    moved_beside = partner_swap(moved_pack, 1)
+    moved_above = partner_swap(moved_pack, 2)
+    state = near(turned_here, here, beside, above)
+    attended = far(turned_here, here, first_half, second_half, state, rows)
+    passed = section_shift(attended)
+    moved_first = partner_swap(moved_beside[:half], 2)
+    moved_second = partner_swap(moved_above[half : 2 * half], 1)
+    state = near(moved_query, moved_pack, moved_beside, moved_above)
+    return far(moved_query, moved_pack, moved_first, moved_second, state, rows, passed)[None]
+
+
 def solution(mesh):
+    if mesh.shape["sp"] != 4:
+        return jax.shard_map(
+            head_exchange, mesh=mesh, in_specs=SPECS, out_specs=SPECS[0], check_vma=False
+        )
+
     return jax.shard_map(
         on_device,
         mesh=mesh,
-        in_specs=(
-            P("section", "sp", None),
-            P("section", "sp", None),
-            P("section", "sp", None, None),
-            P("section"),
-            P("section"),
-        ),
-        out_specs=P("section", "sp", None),
+        in_specs=SPECS,
+        out_specs=SPECS[0],
         check_vma=False,
     )

time: 163 us -> 50.8 us (0.31)
  waiting for transfers between devices: 48.4 us -> 18.6 us
  matrix products: 29.1 us -> 0 us
  other arithmetic: 27.8 us -> 0.42 us
  blocking collectives: 25.7 us -> 0 us
  local copies, waits for them, and re-layouts: 21 us -> 2.17 us
  Pallas kernels: 0 us -> 14.2 us
  starting transfers between devices: 8.86 us -> 13.8 us
    dot_general x64 -> x0, matrix products: 29.1 us -> none  [the longest x16 16.4 us: attend_head(): jnp.dot(own_weights.astype(jnp.bfloat16), value_rows[:key_reach], preferr...]
    all_to_all x1 -> x0, blocking collectives: 25.7 us -> none  [on_device(): lax.all_to_all(passed, 'sp', split_axis=0, concat_axis=1, tiled=True)]
    all_to_all x2 -> x0, waiting for transfers between devices: 21.1 us -> none  [the longest x1 19.2 us: on_device(): lax.all_to_all(local_queries, 'sp', split_axis=1, concat_axis=0, tiled=True)]
    pallas_call x0 -> x6, Pallas kernels: none -> 14.2 us  [the longest x2 7.34 us: near(): pl.pallas_call(near_kernel, out_shape=[jax.ShapeDtypeStruct((turned.shape...]
    ppermute x1 -> x11, starting transfers between devices: 0.06 us -> 13.8 us  [the longest x8 11.8 us: partner_swap(): return lax.ppermute(value, 'sp', [(i, i ^ bits) for i in range(count)])]
    lt x16 -> x0, other arithmetic: 10.4 us -> none  [attend_head(): cache_live = jnp.arange(cache_keys.shape[0], dtype=jnp.int32) < length]
    another operation x17 -> x0, other arithmetic: 10.3 us -> none
    all_to_all x2 -> x0, starting transfers between devices: 8.8 us -> none  [the longest x1 5.19 us: on_device(): lax.all_to_all(broadened, 'sp', split_axis=1, concat_axis=0, tiled=True)]
  transfers between devices with their start and end apart: 3 -> 11, of which waited for: 3 -> 6; matrix products, arithmetic and copies ran while one was open for 6% -> 0% of each run, Pallas kernels for 0% -> 21%
where the time goes in v1:
time: 50.8 us; the launch traced here: 50.6 us
  waiting for transfers between devices  18.6 us (37%)
  Pallas kernels  14.2 us (28%)
  starting transfers between devices  13.8 us (27%)
  local copies, waits for them, and re-layouts  2.17 us (4%)
  between operations  1.42 us (3%)
    ppermute x8, waiting for transfers between devices, partner_swap(): return lax.ppermute(value, 'sp', [(i, i ^ bits) for i in range(count)])  18.6 us
    ppermute x8, starting transfers between devices, partner_swap(): return lax.ppermute(value, 'sp', [(i, i ^ bits) for i in range(count)])  11.8 us
    pallas_call x2, Pallas kernels, near(): pl.pallas_call(near_kernel, out_shape=[jax.ShapeDtypeStruct((turned.shape...  7.34 us
    pallas_call x2, Pallas kernels, far(): pl.pallas_call(far_kernel, out_shape=jax.ShapeDtypeStruct((rows, width *...  5.58 us
    unnamed x6, local copies, waits for them, and re-layouts  2.12 us
    ppermute x3, starting transfers between devices, section_shift(): lax.ppermute(value, 'section', [(i, (i + 1) % count) for i in range(count)])  1.98 us
    pallas_call x1, Pallas kernels, on_device(): pl.pallas_call(turn_kernel, out_shape=[jax.ShapeDtypeStruct((query.size /...  1.03 us
  transfers between devices with their start and end apart: 11, of which 6 were waited for; matrix products, arithmetic and copies ran while one was open for 0% of the time, Pallas kernels for 21%

profile of v1, /device:TPU:0, one launch (start us, length us, event | category | flops | bytes accessed | tf_op | source)
XLA Modules:
  0.0 50.6 jit_solution(9893927983820369188)
XLA Ops:
  1.3 0.3 fusion
  1.6 0.0 copy-start
  1.7 0.1 pad_maximum_fusion
  1.8 0.0 copy-start.1
  1.8 1.2 %copy-done.1 = bf16[1,128,2048]{2,1,0:T(8,128)(2,1)S(1)} copy-done((bf16[1,128,2048]{2,1,0:T(8,128)(2,1)S(1)}, bf16[1,128,2048]{2,1,0:T(8,128)(2,1)}, u32[]{:S(2)}) %copy-start.1) | copy-done | bytes 524312
  2.9 0.0 copy-start.2
  2.9 0.9 %copy-done.2 = bf16[1,2,256,256]{3,2,1,0:T(8,128)(2,1)S(1)} copy-done((bf16[1,2,256,256]{3,2,1,0:T(8,128)(2,1)S(1)}, bf16[1,2,256,256]{3,2,1,0:T(8,128)(2,1)}, u32[]{:S(2)}) %copy-start.2) | copy-done | bytes 262168
  3.9 0.2 shard_map.56
  4.1 3.0 %collective-permute-start.6 = (bf16[784,256]{1,0:T(8,128)(2,1)S(1)}, bf16[784,256]{1,0:T(8,128)(2,1)S(1)}, u32[]{:S(2)}, u32[]{:S(2)}) collective-permute-start(bf16[784,256]{1,0:T(8,128)(2,1)S(1)} %get-tuple-element.18.own), channel_id=1, source_target_pairs={{0,1},{1,0},{2,3},{3,2},{4,5},{5,4},{6,7},{7,6},{8,9},{9,8},{10,11... | collective-permute-start | bytes 1204232 | tf_op jit(solution)/shard_map/ppermute | solution.py:38
  7.1 1.5 %collective-permute-start.8 = (bf16[784,256]{1,0:T(8,128)(2,1)S(1)}, bf16[784,256]{1,0:T(8,128)(2,1)S(1)}, u32[]{:S(2)}, u32[]{:S(2)}) collective-permute-start(bf16[784,256]{1,0:T(8,128)(2,1)S(1)} %get-tuple-element.18.own), channel_id=1, source_target_pairs={{0,2},{1,3},{2,0},{3,1},{4,6},{5,7},{6,4},{7,5},{8,10},{9,11},{10,... | collective-permute-start | bytes 1204232 | tf_op jit(solution)/shard_map/ppermute | solution.py:38
  8.7 0.0 collective-permute-start.1
  8.7 0.0 copy-done
  8.7 1.0 %shard_map.55 = (bf16[4096,128]{1,0:T(8,128)(2,1)S(1)}, bf16[4096,128]{1,0:T(8,128)(2,1)S(1)}) custom-call(bf16[128,8192]{1,0:T(8,128)(2,1)S(1)} %bitcast.6, f32[128,128]{1,0:T(8,128)S(1)} %get-tuple-element.24.cosine, f32[128,128]{1,0:T(8,128)S(1)} %get-tuple-element.25.sine), custom_call_target="tpu_custom_call" | custom-call | flops 1073741824 | bytes 8388608 | tf_op jit(solution)/shard_map/pallas_call | solution.py:365
  9.7 1.7 %collective-permute-start = (bf16[4096,128]{1,0:T(8,128)(2,1)S(1)}, bf16[4096,128]{1,0:T(8,128)(2,1)S(1)}, u32[]{:S(2)}, u32[]{:S(2)}) collective-permute-start(bf16[4096,128]{1,0:T(8,128)(2,1)S(1)} %get-tuple-element.13), channel_id=1, source_target_pairs={{0,4},{4,8},{8,12},{12,16},{16,20},{20,24},{24,28},{28,0},{1,5},{5... | collective-permute-start | bytes 3145736 | tf_op jit(solution)/shard_map/ppermute | solution.py:33
  11.4 5.0 %collective-permute-done.6.beside = bf16[784,256]{1,0:T(8,128)(2,1)S(1)} collective-permute-done((bf16[784,256]{1,0:T(8,128)(2,1)S(1)}, bf16[784,256]{1,0:T(8,128)(2,1)S(1)}, u32[]{:S(2)}, u32[]{:S(2)}) %collective-permute-start.6) | collective-permute-done | bytes 401440 | tf_op jit(solution)/shard_map/ppermute | solution.py:38
  16.4 1.8 %collective-permute-start.7 = (bf16[384,256]{1,0:T(8,128)(2,1)S(1)}, bf16[384,256]{1,0:T(8,128)(2,1)S(1)}, u32[]{:S(2)}, u32[]{:S(2)}) collective-permute-start(bf16[384,256]{1,0:T(8,128)(2,1)S(1)} %slice.18), channel_id=1, source_target_pairs={{0,2},{1,3},{2,0},{3,1},{4,6},{5,7},{6,4},{7,5},{8,10},{9,11},{10,... | collective-permute-start | bytes 589832 | tf_op jit(solution)/shard_map/ppermute | solution.py:38
  18.3 0.0 collective-permute-done.8.above
  18.3 1.6 %collective-permute-start.9 = (bf16[384,256]{1,0:T(8,128)(2,1)S(1)}, bf16[384,256]{1,0:T(8,128)(2,1)S(1)}, u32[]{:S(2)}, u32[]{:S(2)}) collective-permute-start(bf16[384,256]{1,0:T(8,128)(2,1)S(1)} %slice.19), channel_id=1, source_target_pairs={{0,1},{1,0},{2,3},{3,2},{4,5},{5,4},{6,7},{7,6},{8,9},{9,8},{10,11... | collective-permute-start | bytes 589832 | tf_op jit(solution)/shard_map/ppermute | solution.py:38
  19.9 3.7 %shard_map.58 = (f32[4096,128]{1,0:T(8,128)S(1)}, f32[4096,256]{1,0:T(8,128)S(1)}) custom-call(bf16[4096,128]{1,0:T(8,128)(2,1)S(1)} %get-tuple-element.17.query, bf16[784,256]{1,0:T(8,128)(2,1)S(1)} %get-tuple-element.18.own, bf16[784,256]{1,0:T(8,128)(2,1)S(1)} %collective-permute-done.6.beside, bf16[784,256]{1,0:T(8,128)(2,1)S(1)} %collective-permute-done.8.above), custom_call_target="tpu_custom_call" | custom-call | flops 3623878656 | bytes 2097152 | tf_op jit(solution)/shard_map/pallas_call | solution.py:210
  23.5 0.0 collective-permute-done.7.first_half
  23.5 0.5 collective-permute-done.9.second_half
  24.0 2.1 %shard_map.59 = bf16[128,4096]{1,0:T(8,128)(2,1)S(1)} custom-call(bf16[4096,128]{1,0:T(8,128)(2,1)S(1)} %get-tuple-element.17.query, bf16[784,256]{1,0:T(8,128)(2,1)S(1)} %get-tuple-element.18.own, bf16[384,256]{1,0:T(8,128)(2,1)S(1)} %collective-permute-done.7.first_half, bf16[384,256]{1,0:T(8,128)(2,1)S(1)} %collective-permute-done.9.second_half, ...), custom_call_target="tpu_custom_call" | custom-call | flops 1207959552 | bytes 2097152 | tf_op jit(solution)/shard_map/pallas_call | solution.py:229
  26.1 0.2 collective-permute-start.10
  26.4 0.0 collective-permute-done.1.own
  26.4 1.6 %collective-permute-start.2 = (bf16[784,256]{1,0:T(8,128)(2,1)S(1)}, bf16[784,256]{1,0:T(8,128)(2,1)S(1)}, u32[]{:S(2)}, u32[]{:S(2)}) collective-permute-start(bf16[784,256]{1,0:T(8,128)(2,1)S(1)} %collective-permute-done.1.own), channel_id=1, source_target_pairs={{0,1},{1,0},{2,3},{3,2},{4,5},{5,4},{6,7},{7,6},{8,9},{9,8},{10,11... | collective-permute-start | bytes 1204232 | tf_op jit(solution)/shard_map/ppermute | solution.py:38
  28.0 0.5 %collective-permute-start.4 = (bf16[784,256]{1,0:T(8,128)(2,1)S(1)}, bf16[784,256]{1,0:T(8,128)(2,1)S(1)}, u32[]{:S(2)}, u32[]{:S(2)}) collective-permute-start(bf16[784,256]{1,0:T(8,128)(2,1)S(1)} %collective-permute-done.1.own), channel_id=1, source_target_pairs={{0,2},{1,3},{2,0},{3,1},{4,6},{5,7},{6,4},{7,5},{8,10},{9,11},{10,... | collective-permute-start | bytes 1204232 | tf_op jit(solution)/shard_map/ppermute | solution.py:38
  28.5 9.5 %collective-permute-done.2.beside = bf16[784,256]{1,0:T(8,128)(2,1)S(1)} collective-permute-done((bf16[784,256]{1,0:T(8,128)(2,1)S(1)}, bf16[784,256]{1,0:T(8,128)(2,1)S(1)}, u32[]{:S(2)}, u32[]{:S(2)}) %collective-permute-start.2) | collective-permute-done | bytes 401440 | tf_op jit(solution)/shard_map/ppermute | solution.py:38
  38.0 1.2 %collective-permute-start.3 = (bf16[384,256]{1,0:T(8,128)(2,1)S(1)}, bf16[384,256]{1,0:T(8,128)(2,1)S(1)}, u32[]{:S(2)}, u32[]{:S(2)}) collective-permute-start(bf16[384,256]{1,0:T(8,128)(2,1)S(1)} %slice.16), channel_id=1, source_target_pairs={{0,2},{1,3},{2,0},{3,1},{4,6},{5,7},{6,4},{7,5},{8,10},{9,11},{10,... | collective-permute-start | bytes 589832 | tf_op jit(solution)/shard_map/ppermute | solution.py:38
  39.2 0.6 %collective-permute-done.4.above = bf16[784,256]{1,0:T(8,128)(2,1)S(1)} collective-permute-done((bf16[784,256]{1,0:T(8,128)(2,1)S(1)}, bf16[784,256]{1,0:T(8,128)(2,1)S(1)}, u32[]{:S(2)}, u32[]{:S(2)}) %collective-permute-start.4) | collective-permute-done | bytes 401440 | tf_op jit(solution)/shard_map/ppermute | solution.py:38
  39.8 0.6 %collective-permute-start.5 = (bf16[384,256]{1,0:T(8,128)(2,1)S(1)}, bf16[384,256]{1,0:T(8,128)(2,1)S(1)}, u32[]{:S(2)}, u32[]{:S(2)}) collective-permute-start(bf16[384,256]{1,0:T(8,128)(2,1)S(1)} %slice.17), channel_id=1, source_target_pairs={{0,1},{1,0},{2,3},{3,2},{4,5},{5,4},{6,7},{7,6},{8,9},{9,8},{10,11... | collective-permute-start | bytes 589832 | tf_op jit(solution)/shard_map/ppermute | solution.py:38
  40.4 0.0 collective-permute-done.query
  40.4 3.7 %shard_map.57 = (f32[4096,128]{1,0:T(8,128)S(1)}, f32[4096,256]{1,0:T(8,128)S(1)}) custom-call(bf16[4096,128]{1,0:T(8,128)(2,1)S(1)} %collective-permute-done.query, bf16[784,256]{1,0:T(8,128)(2,1)S(1)} %collective-permute-done.1.own, bf16[784,256]{1,0:T(8,128)(2,1)S(1)} %collective-permute-done.2.beside, bf16[784,256]{1,0:T(8,128)(2,1)S(1)} %collective-permute-done.4.above), custom_call_target="tpu_custom_call" | custom-call | flops 3623878656 | bytes 2097152 | tf_op jit(solution)/shard_map/pallas_call | solution.py:210
  44.1 1.6 %collective-permute-done.3.first_half = bf16[384,256]{1,0:T(8,128)(2,1)S(1)} collective-permute-done((bf16[384,256]{1,0:T(8,128)(2,1)S(1)}, bf16[384,256]{1,0:T(8,128)(2,1)S(1)}, u32[]{:S(2)}, u32[]{:S(2)}) %collective-permute-start.3) | collective-permute-done | bytes 196640 | tf_op jit(solution)/shard_map/ppermute | solution.py:38
  45.6 1.5 %collective-permute-done.5.second_half = bf16[384,256]{1,0:T(8,128)(2,1)S(1)} collective-permute-done((bf16[384,256]{1,0:T(8,128)(2,1)S(1)}, bf16[384,256]{1,0:T(8,128)(2,1)S(1)}, u32[]{:S(2)}, u32[]{:S(2)}) %collective-permute-start.5) | collective-permute-done | bytes 196640 | tf_op jit(solution)/shard_map/ppermute | solution.py:38
  47.1 0.0 collective-permute-done.10.rest_0_
  47.1 3.5 %shard_map.60 = bf16[128,8192]{1,0:T(8,128)(2,1)} custom-call(bf16[4096,128]{1,0:T(8,128)(2,1)S(1)} %collective-permute-done.query, bf16[784,256]{1,0:T(8,128)(2,1)S(1)} %collective-permute-done.1.own, bf16[384,256]{1,0:T(8,128)(2,1)S(1)} %collective-permute-done.3.first_half, bf16[384,256]{1,0:T(8,128)(2,1)S(1)} %collective-permute-done.5.second_half, ...), custom_call_target="tpu_custom_call" | custom-call | flops 1207959552 | bytes 2097152 | tf_op jit(solution)/shard_map/pallas_call | solution.py:229
  (6 shorter events, 0.1 us)
Async XLA Ops:
  1.6 7.0 %copy-start = (bf16[1,128,8192]{2,1,0:T(8,128)(2,1)S(1)}, bf16[1,128,8192]{2,1,0:T(8,128)(2,1)}, u32[]{:S(2)}) copy-start(bf16[1,128,8192]{2,1,0:T(8,128)(2,1)} %param.5) | copy-start | bytes 6291460
  1.8 1.2 %copy-start.1 = (bf16[1,128,2048]{2,1,0:T(8,128)(2,1)S(1)}, bf16[1,128,2048]{2,1,0:T(8,128)(2,1)}, u32[]{:S(2)}) copy-start(bf16[1,128,2048]{2,1,0:T(8,128)(2,1)} %param.6) | copy-start | bytes 1572868
  2.9 0.9 %copy-start.2 = (bf16[1,2,256,256]{3,2,1,0:T(8,128)(2,1)S(1)}, bf16[1,2,256,256]{3,2,1,0:T(8,128)(2,1)}, u32[]{:S(2)}) copy-start(bf16[1,2,256,256]{3,2,1,0:T(8,128)(2,1)} %param.7) | copy-start | bytes 786436
  4.1 12.3 %collective-permute-start.6 = (bf16[784,256]{1,0:T(8,128)(2,1)S(1)}, bf16[784,256]{1,0:T(8,128)(2,1)S(1)}, u32[]{:S(2)}, u32[]{:S(2)}) collective-permute-start(bf16[784,256]{1,0:T(8,128)(2,1)S(1)} %get-tuple-element.18.own), channel_id=1, source_target_pairs={{0,1},{1,0},{2,3},{3,2},{4,5},{5,4},{6,7},{7,6},{8,9},{9,8},{10,11... | collective-permute-start | bytes 1204232 | tf_op jit(solution)/shard_map/ppermute | solution.py:38
  7.1 11.1 %collective-permute-start.8 = (bf16[784,256]{1,0:T(8,128)(2,1)S(1)}, bf16[784,256]{1,0:T(8,128)(2,1)S(1)}, u32[]{:S(2)}, u32[]{:S(2)}) collective-permute-start(bf16[784,256]{1,0:T(8,128)(2,1)S(1)} %get-tuple-element.18.own), channel_id=1, source_target_pairs={{0,2},{1,3},{2,0},{3,1},{4,6},{5,7},{6,4},{7,5},{8,10},{9,11},{10,... | collective-permute-start | bytes 1204232 | tf_op jit(solution)/shard_map/ppermute | solution.py:38
  8.7 17.7 %collective-permute-start.1 = (bf16[784,256]{1,0:T(8,128)(2,1)S(1)}, bf16[784,256]{1,0:T(8,128)(2,1)S(1)}, u32[]{:S(2)}, u32[]{:S(2)}) collective-permute-start(bf16[784,256]{1,0:T(8,128)(2,1)S(1)} %get-tuple-element.14), channel_id=1, source_target_pairs={{0,4},{4,8},{8,12},{12,16},{16,20},{20,24},{24,28},{28,0},{1,5},{5... | collective-permute-start | bytes 1204232 | tf_op jit(solution)/shard_map/ppermute | solution.py:33
  9.7 30.7 %collective-permute-start = (bf16[4096,128]{1,0:T(8,128)(2,1)S(1)}, bf16[4096,128]{1,0:T(8,128)(2,1)S(1)}, u32[]{:S(2)}, u32[]{:S(2)}) collective-permute-start(bf16[4096,128]{1,0:T(8,128)(2,1)S(1)} %get-tuple-element.13), channel_id=1, source_target_pairs={{0,4},{4,8},{8,12},{12,16},{16,20},{20,24},{24,28},{28,0},{1,5},{5... | collective-permute-start | bytes 3145736 | tf_op jit(solution)/shard_map/ppermute | solution.py:33
  16.4 7.1 %collective-permute-start.7 = (bf16[384,256]{1,0:T(8,128)(2,1)S(1)}, bf16[384,256]{1,0:T(8,128)(2,1)S(1)}, u32[]{:S(2)}, u32[]{:S(2)}) collective-permute-start(bf16[384,256]{1,0:T(8,128)(2,1)S(1)} %slice.18), channel_id=1, source_target_pairs={{0,2},{1,3},{2,0},{3,1},{4,6},{5,7},{6,4},{7,5},{8,10},{9,11},{10,... | collective-permute-start | bytes 589832 | tf_op jit(solution)/shard_map/ppermute | solution.py:38
  18.3 5.7 %collective-permute-start.9 = (bf16[384,256]{1,0:T(8,128)(2,1)S(1)}, bf16[384,256]{1,0:T(8,128)(2,1)S(1)}, u32[]{:S(2)}, u32[]{:S(2)}) collective-permute-start(bf16[384,256]{1,0:T(8,128)(2,1)S(1)} %slice.19), channel_id=1, source_target_pairs={{0,1},{1,0},{2,3},{3,2},{4,5},{5,4},{6,7},{7,6},{8,9},{9,8},{10,11... | collective-permute-start | bytes 589832 | tf_op jit(solution)/shard_map/ppermute | solution.py:38
  26.1 21.0 %collective-permute-start.10 = (bf16[128,4096]{1,0:T(8,128)(2,1)S(1)}, bf16[128,4096]{1,0:T(8,128)(2,1)S(1)}, u32[]{:S(2)}, u32[]{:S(2)}) collective-permute-start(bf16[128,4096]{1,0:T(8,128)(2,1)S(1)} %shard_map.59), channel_id=1, source_target_pairs={{0,4},{4,8},{8,12},{12,16},{16,20},{20,24},{24,28},{28,0},{1,5},{5... | collective-permute-start | bytes 3145736 | tf_op jit(solution)/shard_map/ppermute | solution.py:33
  26.4 11.6 %collective-permute-start.2 = (bf16[784,256]{1,0:T(8,128)(2,1)S(1)}, bf16[784,256]{1,0:T(8,128)(2,1)S(1)}, u32[]{:S(2)}, u32[]{:S(2)}) collective-permute-start(bf16[784,256]{1,0:T(8,128)(2,1)S(1)} %collective-permute-done.1.own), channel_id=1, source_target_pairs={{0,1},{1,0},{2,3},{3,2},{4,5},{5,4},{6,7},{7,6},{8,9},{9,8},{10,11... | collective-permute-start | bytes 1204232 | tf_op jit(solution)/shard_map/ppermute | solution.py:38
  28.0 11.8 %collective-permute-start.4 = (bf16[784,256]{1,0:T(8,128)(2,1)S(1)}, bf16[784,256]{1,0:T(8,128)(2,1)S(1)}, u32[]{:S(2)}, u32[]{:S(2)}) collective-permute-start(bf16[784,256]{1,0:T(8,128)(2,1)S(1)} %collective-permute-done.1.own), channel_id=1, source_target_pairs={{0,2},{1,3},{2,0},{3,1},{4,6},{5,7},{6,4},{7,5},{8,10},{9,11},{10,... | collective-permute-start | bytes 1204232 | tf_op jit(solution)/shard_map/ppermute | solution.py:38
  38.0 7.6 %collective-permute-start.3 = (bf16[384,256]{1,0:T(8,128)(2,1)S(1)}, bf16[384,256]{1,0:T(8,128)(2,1)S(1)}, u32[]{:S(2)}, u32[]{:S(2)}) collective-permute-start(bf16[384,256]{1,0:T(8,128)(2,1)S(1)} %slice.16), channel_id=1, source_target_pairs={{0,2},{1,3},{2,0},{3,1},{4,6},{5,7},{6,4},{7,5},{8,10},{9,11},{10,... | collective-permute-start | bytes 589832 | tf_op jit(solution)/shard_map/ppermute | solution.py:38
  39.8 7.3 %collective-permute-start.5 = (bf16[384,256]{1,0:T(8,128)(2,1)S(1)}, bf16[384,256]{1,0:T(8,128)(2,1)S(1)}, u32[]{:S(2)}, u32[]{:S(2)}) collective-permute-start(bf16[384,256]{1,0:T(8,128)(2,1)S(1)} %slice.17), channel_id=1, source_target_pairs={{0,1},{1,0},{2,3},{3,2},{4,5},{5,4},{6,7},{7,6},{8,9},{9,8},{10,11... | collective-permute-start | bytes 589832 | tf_op jit(solution)/shard_map/ppermute | solution.py:38

commit v2 on v1

--- a/solution.py
+++ b/solution.py
@@ -1,3 +1,4 @@
+import functools
 import math
 
 import jax
@@ -25,12 +26,14 @@
     P("section"),
 )
 VMEM = pl.BlockSpec(memory_space=pltpu.VMEM)
+HBM = pl.BlockSpec(memory_space=pltpu.HBM)
 LIMIT = pltpu.CompilerParams(vmem_limit_bytes=20 * 2**20)
 
 
-def section_shift(value):
+def section_shift(value, side=None):
     count = lax.axis_size("section")
-    return lax.ppermute(value, "section", [(i, (i + 1) % count) for i in range(count)])
+    pairs = [(i, (i + 1) % count) for i in range(count) if side is None or i % 2 == side]
+    return lax.ppermute(value, "section", pairs)
 
 
 def partner_swap(value, bits):
@@ -46,32 +49,57 @@
     return (jnp.cos(angle), jnp.sin(angle))
 
 
+def rotation_frequency(head_width):
+    exponent = jnp.arange(head_width // 2, dtype=jnp.float32) * (-2.0 / head_width)
+    frequency = jnp.power(jnp.float32(ROPE_BASE), exponent)
+    return jnp.concatenate([frequency, frequency])
+
+
 def rotated(value, cosine, sine):
     wide = value.astype(jnp.float32)
     turned = pltpu.roll(wide, HEAD_SIZE // 2, 1)
     return (wide * cosine + turned * sine).astype(jnp.bfloat16)
 
 
-def pack_kernel(keyval, cache, cosine, sine, length, *packs):
-    rows = keyval.shape[0]
+def pack_kernel(
+    keyval, cache, offsets, lengths, frequency, *rest
+):
+    packs, (cosine, sine, loaded, offset, length, sem) = rest[:-6], rest[-6:]
+    rows, positions = keyval.shape[0], cache.shape[1]
+    heads = KEY_VALUE_HEADS // len(packs)
+    middle = heads // 2 * rows
+    last = heads * rows + positions
+    moves = [(offsets, offset), (lengths, length), (keyval, loaded)]
+    for chunk, pack in enumerate(packs):
+        moves.append((cache.at[chunk], pack.at[middle : middle + positions]))
+    copies = [
+        pltpu.make_async_copy(source, target, sem.at[place])
+        for place, (source, target) in enumerate(moves)
+    ]
+    for copy in copies:
+        copy.start()
+    copies[0].wait()
+    first = offset[0] + lax.axis_index("sp") * rows
+    place = first + lax.broadcasted_iota(jnp.int32, cosine.shape, 0)
+    angle = place.astype(jnp.float32) * frequency[...]
+    low = lax.broadcasted_iota(jnp.int32, cosine.shape, 1) < HEAD_SIZE // 2
+    cosine[...] = jnp.cos(angle)
+    turn = jnp.sin(angle)
+    sine[...] = jnp.where(low, -turn, turn)
+    for copy in copies[1:]:
+        copy.wait()
     cos_here, sin_here = cosine[...], sine[...]
-    positions = cache.shape[1]
     live = length[0].astype(jnp.float32)
     for chunk, pack in enumerate(packs):
-        heads = KEY_VALUE_HEADS // len(packs)
         for index in range(heads):
-            head = index * len(packs) + chunk
             start = index * rows + (positions if index >= heads // 2 else 0)
-            column = head * 2 * HEAD_SIZE
+            column = (index * len(packs) + chunk) * 2 * HEAD_SIZE
             pack[start : start + rows, :HEAD_SIZE] = rotated(
-                keyval[:, column : column + HEAD_SIZE], cos_here, sin_here
+                loaded[:, column : column + HEAD_SIZE], cos_here, sin_here
             )
-            pack[start : start + rows, HEAD_SIZE:] = keyval[
+            pack[start : start + rows, HEAD_SIZE:] = loaded[
                 :, column + HEAD_SIZE : column + 2 * HEAD_SIZE
             ]
-        middle = heads // 2 * rows
-        pack[middle : middle + positions, :] = cache[chunk]
-        last = heads * rows + positions
         pack[last:, :] = jnp.full((pack.shape[0] - last, pack.shape[1]), live, jnp.float32).astype(
             jnp.bfloat16
         )
@@ -110,13 +138,32 @@
     return place < length[:, :positions]
 
 
-def near_kernel(query, own, beside, above, top_ref, sums_ref):
+def run_on_side(body, side, *refs):
+    if side is None:
+        body(*refs)
+    else:
+        pl.when(lax.axis_index("section") % 2 == side)(lambda: body(*refs))
+
+
+def stored_parts(parts):
+    keys = jnp.concatenate([part[:, :HEAD_SIZE] for part in parts], axis=0)
+    return keys, jnp.concatenate([part[:, HEAD_SIZE:] for part in parts], axis=0)
+
+
+def near_kernel(rows, side, *refs):
+    run_on_side(functools.partial(near_body, rows), side, *refs)
+
+
+def near_body(rows, query, own, *rest):
+    halves, (top_ref, sums_ref, beside, above) = rest[:4], rest[4:]
     me = lax.axis_index("sp")
-    total = query.shape[0]
-    rows = 128
-    heads = total // (GROUP * rows)
+    heads = query.shape[0] // (GROUP * rows)
     positions = own.shape[0] - 16 - heads * rows
     middle = heads // 2 * rows
+    half = halves[0].shape[0]
+    for block, first, second in ((beside, *halves[:2]), (above, *halves[2:])):
+        block[:half, :] = first[...]
+        block[half:, :] = second[: block.shape[0] - half, :]
     blocks = (own, beside, above)
     live = live_mask(own, positions)
     step_rows = STEP_HEADS * rows
@@ -127,116 +174,149 @@
     for offset in range(len(blocks) + 1):
         head = me ^ offset
         start = pl.multiple_of(head * rows + jnp.where(head >= heads // 2, positions, 0), rows)
-        stored = [block[pl.ds(start, rows), :] for block in blocks]
+        parts = [block[pl.ds(start, rows), :] for block in blocks]
         if offset < len(blocks):
-            stored.append(blocks[offset][middle : middle + positions, :])
-        keys = jnp.concatenate([part[:, :HEAD_SIZE] for part in stored], axis=0)
-        values = jnp.concatenate([part[:, HEAD_SIZE:] for part in stored], axis=0)
+            parts.append(blocks[offset][middle : middle + positions, :])
+        keys, values = stored_parts(parts)
         base = pl.multiple_of(head * (GROUP * rows), rows)
         for step in range(GROUP // STEP_HEADS):
             place = pl.ds(base + step * step_rows, step_rows)
             scores = dot_scores(query[place, :], keys)
-            parts = [jnp.where(causal, scores[:, :rows], MASKED)]
+            pieces = [jnp.where(causal, scores[:, :rows], MASKED)]
             for other in range(1, len(blocks)):
                 piece = scores[:, other * rows : (other + 1) * rows]
-                parts.append(jnp.where((me ^ other) < me, piece, MASKED))
+                pieces.append(jnp.where((me ^ other) < me, piece, MASKED))
             if offset < len(blocks):
-                parts.append(jnp.where(live, scores[:, len(blocks) * rows :], MASKED))
-            scores = jnp.concatenate(parts, axis=1)
+                pieces.append(jnp.where(live, scores[:, len(blocks) * rows :], MASKED))
+            scores = jnp.concatenate(pieces, axis=1)
             top = jnp.max(scores, axis=1, keepdims=True)
             weights = jnp.exp2((scores - top) * FACTOR).astype(jnp.bfloat16)
             sums_ref[place, :] = weighted(weights, values)
             top_ref[place, :] = jnp.broadcast_to(top, (step_rows, HEAD_SIZE))
 
 
-def far_kernel(query, own, first_half, second_half, top_ref, sums_ref, *rest):
-    passed, out, across = rest if len(rest) == 3 else (None, *rest)
+def far_kernel(rows, stride, side, *refs):
+    run_on_side(functools.partial(far_body, rows, stride), side, *refs)
+
+
+def far_body(rows, stride, query, own, first_half, second_half, top_ref, sums_ref, *rest):
+    out, across, results, sem = rest if len(rest) == 4 else (*rest, None, None)
     me = lax.axis_index("sp")
-    rows = out.shape[0]
     heads = query.shape[0] // (GROUP * rows)
     half = first_half.shape[0]
     positions = 2 * half - heads * rows
     middle = heads // 2 * rows
     width = GROUP * HEAD_SIZE
     across[:half, :] = first_half[...]
-    across[half:, :] = second_half[...]
+    across[half:, :] = second_half[: across.shape[0] - half, :]
     live = live_mask(own, positions)
     step_rows = STEP_HEADS * rows
     far = heads - 1
-    if passed is not None:
-        for index in range(heads):
-            out[:, 2 * index * width : (2 * index + 1) * width] = passed[
-                :, index * width : (index + 1) * width
-            ]
+    copies = []
     for offset in range(heads):
         head = me ^ offset
         start = pl.multiple_of(head * rows + jnp.where(head >= heads // 2, positions, 0), rows)
-        stored = [across[pl.ds(start, rows), :]]
+        parts = [across[pl.ds(start, rows), :]]
         if offset == far:
-            stored.append(across[middle : middle + positions, :])
-        keys = jnp.concatenate([part[:, :HEAD_SIZE] for part in stored], axis=0)
-        values = jnp.concatenate([part[:, HEAD_SIZE:] for part in stored], axis=0)
+            parts.append(across[middle : middle + positions, :])
+        keys, values = stored_parts(parts)
         base = pl.multiple_of(head * (GROUP * rows), rows)
         for step in range(GROUP // STEP_HEADS):
             place = pl.ds(base + step * step_rows, step_rows)
             scores = dot_scores(query[place, :], keys)
-            parts = [jnp.where((me ^ far) < me, scores[:, :rows], MASKED)]
+            pieces = [jnp.where((me ^ far) < me, scores[:, :rows], MASKED)]
             if offset == far:
-                parts.append(jnp.where(live, scores[:, rows:], MASKED))
-            scores = jnp.concatenate(parts, axis=1)
+                pieces.append(jnp.where(live, scores[:, rows:], MASKED))
+            scores = jnp.concatenate(pieces, axis=1)
             before = top_ref[place, :]
             top = jnp.maximum(jnp.max(scores, axis=1, keepdims=True), before)
             kept = jnp.exp2((before - top) * FACTOR)
-            weights = jnp.exp2(
-                (scores - jnp.concatenate([top] * len(parts[:1] + parts[1:] * 2), axis=1)) * FACTOR
-            ).astype(jnp.bfloat16)
+            wide_top = jnp.concatenate([top] * (scores.shape[1] // HEAD_SIZE), axis=1)
+            weights = jnp.exp2((scores - wide_top) * FACTOR).astype(jnp.bfloat16)
             sums = weighted(weights, values) + sums_ref[place, :] * jnp.concatenate(
                 [kept, kept], axis=1
             )
             result = (sums[:, :HEAD_SIZE] / sums[:, HEAD_SIZE:]).astype(jnp.bfloat16)
             for part in range(STEP_HEADS):
                 lane = (step * STEP_HEADS + part) * HEAD_SIZE
-                if passed is None:
-                    column = head * width + lane
+                piece = result[part * rows : (part + 1) * rows]
+                if results is None:
+                    column = pl.multiple_of(head * width + lane, HEAD_SIZE)
+                    out[:, pl.ds(column, HEAD_SIZE)] = piece
                 else:
-                    column = (2 * head + 1) * width + lane
-                out[:, pl.ds(pl.multiple_of(column, HEAD_SIZE), HEAD_SIZE)] = result[
-                    part * rows : (part + 1) * rows
-                ]
-
-
-def near(turned, own, beside, above):
-    work = turned.shape[0] * 576
+                    results[offset, :, lane : lane + HEAD_SIZE] = piece
+        if results is not None:
+            column = pl.multiple_of((stride * head + stride - 1) * width, width)
+            copy = pltpu.make_async_copy(
+                results.at[offset], out.at[:, pl.ds(column, width)], sem.at[offset]
+            )
+            copy.start()
+            copies.append(copy)
+    for copy in copies:
+        copy.wait()
+
+
+def join_kernel(from_odd, from_even, before, out, sem):
+    width = GROUP * HEAD_SIZE
+
+    def place(passed):
+        copies = []
+        for index in range(passed.shape[1] // width):
+            copies.append(
+                pltpu.make_async_copy(
+                    passed.at[:, index * width : (index + 1) * width],
+                    out.at[:, 2 * index * width : (2 * index + 1) * width],
+                    sem.at[index],
+                )
+            )
+        for copy in copies:
+            copy.start()
+        for copy in copies:
+            copy.wait()
+
+    for passed, side in ((from_odd, 0), (from_even, 1)):
+        run_on_side(place, side, passed)
+
+
+def near(turned, rows, own, beside, above, side=None):
+    block = pltpu.VMEM((own.shape[0] - 16, own.shape[1]), jnp.bfloat16)
+    work = turned.shape[0] * 5 * rows
     return pl.pallas_call(
-        near_kernel,
+        functools.partial(near_kernel, rows, side),
         out_shape=[
-            jax.ShapeDtypeStruct((turned.shape[0], HEAD_SIZE), jnp.float32),
-            jax.ShapeDtypeStruct((turned.shape[0], 2 * HEAD_SIZE), jnp.float32),
+            pltpu.VMEM((turned.shape[0], HEAD_SIZE), jnp.float32),
+            pltpu.VMEM((turned.shape[0], 2 * HEAD_SIZE), jnp.float32),
         ],
-        in_specs=[VMEM] * 4,
+        in_specs=[VMEM] * 6,
         out_specs=[VMEM] * 2,
+        scratch_shapes=[block] * 2,
         compiler_params=LIMIT,
         cost_estimate=pl.CostEstimate(
             flops=12 * work * HEAD_SIZE, bytes_accessed=4 * turned.size, transcendentals=work
         ),
-    )(turned, own, beside, above)
-
-
-def far(turned, own, first_half, second_half, state, rows, passed=None):
-    work = turned.shape[0] * 192
+    )(turned, own, *beside, *above)
+
+
+def far(turned, rows, own, first_half, second_half, state, stride=1, side=None):
+    work = turned.shape[0] * 2 * rows
     width = turned.shape[0] // rows * HEAD_SIZE
-    extra = [] if passed is None else [passed]
+    heads = width // (GROUP * HEAD_SIZE)
+    scratch = [pltpu.VMEM((2 * first_half.shape[0], 2 * HEAD_SIZE), jnp.bfloat16)]
+    if stride > 1:
+        scratch.append(pltpu.VMEM((heads, rows, GROUP * HEAD_SIZE), jnp.bfloat16))
+        scratch.append(pltpu.SemaphoreType.DMA((heads,)))
+    place = pltpu.VMEM if stride == 1 else pltpu.HBM
     return pl.pallas_call(
-        far_kernel,
-        out_shape=jax.ShapeDtypeStruct((rows, width * (1 + len(extra))), jnp.bfloat16),
-        in_specs=[VMEM] * (6 + len(extra)),
-        out_specs=VMEM,
-        scratch_shapes=[pltpu.VMEM((2 * first_half.shape[0], own.shape[1]), jnp.bfloat16)],
+        functools.partial(far_kernel, rows, stride, side),
+        out_shape=place((rows, width * stride), jnp.bfloat16),
+        in_specs=[VMEM] * 6,
+        out_specs=pl.BlockSpec(memory_space=place),
+        scratch_shapes=scratch,
         compiler_params=LIMIT,
         cost_estimate=pl.CostEstimate(
             flops=12 * work * HEAD_SIZE, bytes_accessed=4 * turned.size, transcendentals=work
         ),
-    )(turned, own, first_half, second_half, *state, *extra)
+    )(turned, own, first_half, second_half, *state)
 
 
 def passed_along(value, axis, steps):
@@ -348,46 +428,66 @@
     rows = query.shape[1]
     chunks = cache.shape[1]
     heads = KEY_VALUE_HEADS // chunks
-    positions = offsets[0] + lax.axis_index("sp") * rows + jnp.arange(rows, dtype=jnp.int32)
-    cosine, sine = rotation_tables(positions, HEAD_SIZE)
-    cosine = jnp.concatenate([cosine, cosine], axis=1)
-    sine = jnp.concatenate([-sine, sine], axis=1)
-    pack_rows = heads * rows + cache.shape[2] + 16
-    half = (pack_rows - 16) // 2
-    here, ahead = pl.pallas_call(
+    half = (heads * rows + cache.shape[2]) // 2
+    pack = pltpu.VMEM((2 * half + 16, 2 * HEAD_SIZE), jnp.bfloat16)
+    table = pltpu.VMEM((rows, HEAD_SIZE), jnp.float32)
+    items = [pltpu.with_memory_space_constraint(x, pltpu.HBM) for x in (keyval[0], cache[0])]
+    items += [offsets, lengths]
+    here, ahead, cosine, sine = pl.pallas_call(
         pack_kernel,
-        out_shape=[jax.ShapeDtypeStruct((pack_rows, 2 * HEAD_SIZE), jnp.bfloat16)] * chunks,
-        in_specs=[VMEM] * 4 + [pl.BlockSpec(memory_space=pltpu.SMEM)],
-        out_specs=[VMEM] * chunks,
+        out_shape=[pack] * chunks + [table] * 2,
+        in_specs=[HBM] * 4 + [VMEM],
+        out_specs=[VMEM] * (chunks + 2),
+        scratch_shapes=[
+            pltpu.VMEM(keyval.shape[1:], jnp.bfloat16),
+            pltpu.SMEM((1,), jnp.int32),
+            pltpu.SMEM((1,), jnp.int32),
+            pltpu.SemaphoreType.DMA((3 + chunks,)),
+        ],
         compiler_params=LIMIT,
         cost_estimate=pl.CostEstimate(flops=2**30, bytes_accessed=2**21, transcendentals=0),
-    )(keyval[0], cache[0], cosine, sine, lengths)
+    )(*items, rotation_frequency(HEAD_SIZE)[None])
+    turned = pltpu.VMEM((query.size // (HEAD_SIZE * chunks), HEAD_SIZE), jnp.bfloat16)
     turned_here, turned_ahead = pl.pallas_call(
         turn_kernel,
-        out_shape=[
-            jax.ShapeDtypeStruct((query.size // (HEAD_SIZE * chunks), HEAD_SIZE), jnp.bfloat16)
-        ]
-        * chunks,
+        out_shape=[turned] * chunks,
         in_specs=[VMEM] * 3,
         out_specs=[VMEM] * chunks,
         compiler_params=LIMIT,
         cost_estimate=pl.CostEstimate(flops=2**30, bytes_accessed=2**23, transcendentals=0),
     )(query[0], cosine, sine)
-    beside = partner_swap(here, 1)
-    above = partner_swap(here, 2)
+    beside = [partner_swap(here[:half], 1)]
+    above = [partner_swap(here[half:], 2)]
+    beside.append(partner_swap(here[half:], 1))
+    above.insert(0, partner_swap(here[:half], 2))
     moved_pack = section_shift(ahead)
     moved_query = section_shift(turned_ahead)
-    first_half = partner_swap(beside[:half], 2)
-    second_half = partner_swap(above[half : 2 * half], 1)
-    moved_beside = partner_swap(moved_pack, 1)
-    moved_above = partner_swap(moved_pack, 2)
-    state = near(turned_here, here, beside, above)
-    attended = far(turned_here, here, first_half, second_half, state, rows)
-    passed = section_shift(attended)
-    moved_first = partner_swap(moved_beside[:half], 2)
-    moved_second = partner_swap(moved_above[half : 2 * half], 1)
-    state = near(moved_query, moved_pack, moved_beside, moved_above)
-    return far(moved_query, moved_pack, moved_first, moved_second, state, rows, passed)[None]
+    first_half = partner_swap(beside[0], 2)
+    second_half = partner_swap(above[1], 1)
+    moved_beside = [partner_swap(moved_pack[:half], 1)]
+    moved_above = [partner_swap(moved_pack[half:], 2)]
+    moved_beside.append(partner_swap(moved_pack[half:], 1))
+    moved_above.insert(0, partner_swap(moved_pack[:half], 2))
+    state = near(turned_here, rows, here, beside, above)
+    passed = []
+    for side in (1, 0):
+        attended = far(turned_here, rows, here, first_half, second_half, state, side=side)
+        passed.append(section_shift(attended, side))
+    moved_first = partner_swap(moved_beside[0], 2)
+    moved_second = partner_swap(moved_above[1], 1)
+    state = near(moved_query, rows, moved_pack, moved_beside, moved_above)
+    out = far(moved_query, rows, moved_pack, moved_first, moved_second, state, chunks)
+    out = pl.pallas_call(
+        join_kernel,
+        out_shape=pltpu.HBM(out.shape, out.dtype),
+        in_specs=[VMEM, VMEM, HBM],
+        out_specs=HBM,
+        scratch_shapes=[pltpu.SemaphoreType.DMA((heads,))],
+        input_output_aliases={2: 0},
+        compiler_params=LIMIT,
+        cost_estimate=pl.CostEstimate(flops=2**20, bytes_accessed=2**21, transcendentals=0),
+    )(*passed, out)
+    return out[None]
 
 
 def solution(mesh):

time: 50.8 us -> 54.2 us (1.067)
  starting transfers between devices: 13.8 us -> 21.1 us
  waiting for transfers between devices: 18.6 us -> 15.6 us
  local copies, waits for them, and re-layouts: 2.17 us -> 0.06 us
  Pallas kernels: 14.2 us -> 15.6 us
    ppermute x8 -> x12, starting transfers between devices: 11.8 us -> 16.9 us  [partner_swap(): return lax.ppermute(value, 'sp', [(i, i ^ bits) for i in range(count)])]
    ppermute x8 -> x12, waiting for transfers between devices: 18.6 us -> 15.5 us  [partner_swap(): return lax.ppermute(value, 'sp', [(i, i ^ bits) for i in range(count)])]
    ppermute x3 -> x4, starting transfers between devices: 1.98 us -> 4.28 us  [section_shift(): return lax.ppermute(value, 'section', pairs)]
    unnamed x6 -> x2, local copies, waits for them, and re-layouts: 2.12 us -> 0.01 us
    pallas_call x6 -> x8, Pallas kernels: 14.2 us -> 15.6 us  [the longest x2 7.35 us: near(): pl.pallas_call(functools.partial(near_kernel, rows, side), out_shape=[plt...]
  transfers between devices with their start and end apart: 11 -> 16, of which waited for: 6 -> 6; matrix products, arithmetic and copies ran while one was open for 0% -> 0% of each run, Pallas kernels for 21% -> 24%
where the time goes in v2:
time: 54.2 us; the launch traced here: 54 us
  starting transfers between devices  21.1 us (39%)
  Pallas kernels  15.6 us (29%)
  waiting for transfers between devices  15.6 us (29%)
  between operations  1.6 us (3%)
    ppermute x12, starting transfers between devices, partner_swap(): return lax.ppermute(value, 'sp', [(i, i ^ bits) for i in range(count)])  16.9 us
    ppermute x12, waiting for transfers between devices, partner_swap(): return lax.ppermute(value, 'sp', [(i, i ^ bits) for i in range(count)])  15.5 us
    pallas_call x2, Pallas kernels, near(): pl.pallas_call(functools.partial(near_kernel, rows, side), out_shape=[plt...  7.35 us
    pallas_call x3, Pallas kernels, far(): pl.pallas_call(functools.partial(far_kernel, rows, stride, side), out_sha...  4.68 us
    ppermute x4, starting transfers between devices, section_shift(): return lax.ppermute(value, 'section', pairs)  4.28 us
    pallas_call x1, Pallas kernels, on_device(): pl.pallas_call(pack_kernel, out_shape=[pack] * chunks + [table] * 2, in_s...  1.49 us
  transfers between devices with their start and end apart: 16, of which 6 were waited for; matrix products, arithmetic and copies ran while one was open for 0% of the time, Pallas kernels for 24%

profile of v2, /device:TPU:0, one launch (start us, length us, event | category | flops | bytes accessed | tf_op | source)
XLA Modules:
  0.0 54.0 jit_solution(1127176920106177382)
XLA Ops:
  1.3 0.1 maximum_bitcast_fusion.frequency
  1.4 0.0 copy-start
  1.4 1.5 %shard_map.55 = (bf16[784,256]{1,0:T(8,128)(2,1)S(1)}, bf16[784,256]{1,0:T(8,128)(2,1)S(1)}, f32[128,128]{1,0:T(8,128)S(1)}, f32[128,128]{1,0:T(8,128)S(1)}) custom-call(bf16[128,2048]{1,0:T(8,128)(2,1)} %bitcast.7, bf16[2,256,256]{2,1,0:T(8,128)(2,1)} %bitcast.8, s32[1]{0:T(128)S(6)} %copy.8.offsets, s32[1]{0:T(128)S(6)} %copy.9.lengths, ...), custom_call_target="tpu_custom_call" | custom-call | flops 1073741824 | bytes 2097152 | tf_op jit(solution)/shard_map/pallas_call | solution.py:436
  2.9 3.1 %collective-permute-start.2 = (bf16[400,256]{1,0:T(8,128)(2,1)S(1)}, bf16[400,256]{1,0:T(8,128)(2,1)S(1)}, u32[]{:S(2)}, u32[]{:S(2)}) collective-permute-start(bf16[400,256]{1,0:T(8,128)(2,1)S(1)} %slice.17), channel_id=1, source_target_pairs={{0,2},{1,3},{2,0},{3,1},{4,6},{5,7},{6,4},{7,5},{8,10},{9,11},{10,... | collective-permute-start | bytes 614408 | tf_op jit(solution)/shard_map/ppermute | solution.py:41
  6.0 1.5 %collective-permute-start.4 = (bf16[400,256]{1,0:T(8,128)(2,1)S(1)}, bf16[400,256]{1,0:T(8,128)(2,1)S(1)}, u32[]{:S(2)}, u32[]{:S(2)}) collective-permute-start(bf16[400,256]{1,0:T(8,128)(2,1)S(1)} %slice.17), channel_id=1, source_target_pairs={{0,1},{1,0},{2,3},{3,2},{4,5},{5,4},{6,7},{7,6},{8,9},{9,8},{10,11... | collective-permute-start | bytes 614408 | tf_op jit(solution)/shard_map/ppermute | solution.py:41
  7.5 0.6 %collective-permute-start = (bf16[384,256]{1,0:T(8,128)(2,1)S(1)}, bf16[384,256]{1,0:T(8,128)(2,1)S(1)}, u32[]{:S(2)}, u32[]{:S(2)}) collective-permute-start(bf16[384,256]{1,0:T(8,128)(2,1)S(1)} %slice.16), channel_id=1, source_target_pairs={{0,1},{1,0},{2,3},{3,2},{4,5},{5,4},{6,7},{7,6},{8,9},{9,8},{10,11... | collective-permute-start | bytes 589832 | tf_op jit(solution)/shard_map/ppermute | solution.py:41
  8.1 0.1 collective-permute-start.5
  8.2 0.0 copy-done
  8.2 1.0 %shard_map.56 = (bf16[4096,128]{1,0:T(8,128)(2,1)S(1)}, bf16[4096,128]{1,0:T(8,128)(2,1)S(1)}) custom-call(bf16[128,8192]{1,0:T(8,128)(2,1)S(1)} %bitcast.6, f32[128,128]{1,0:T(8,128)S(1)} %get-tuple-element.15.cosine, f32[128,128]{1,0:T(8,128)S(1)} %get-tuple-element.16.sine), custom_call_target="tpu_custom_call" | custom-call | flops 1073741824 | bytes 8388608 | tf_op jit(solution)/shard_map/pallas_call | solution.py:451
  9.2 0.1 collective-permute-start.8
  9.3 7.5 %collective-permute-done.refs_2_ = bf16[384,256]{1,0:T(8,128)(2,1)S(1)} collective-permute-done((bf16[384,256]{1,0:T(8,128)(2,1)S(1)}, bf16[384,256]{1,0:T(8,128)(2,1)S(1)}, u32[]{:S(2)}, u32[]{:S(2)}) %collective-permute-start) | collective-permute-done | bytes 196640 | tf_op jit(solution)/shard_map/ppermute | solution.py:41
  16.7 0.0 collective-permute-start.9
  16.7 0.0 collective-permute-done.5.refs_4_
  16.7 0.4 collective-permute-start.1
  17.1 0.0 collective-permute-done.2.refs_5_
  17.1 1.6 %collective-permute-start.3 = (bf16[400,256]{1,0:T(8,128)(2,1)S(1)}, bf16[400,256]{1,0:T(8,128)(2,1)S(1)}, u32[]{:S(2)}, u32[]{:S(2)}) collective-permute-start(bf16[400,256]{1,0:T(8,128)(2,1)S(1)} %collective-permute-done.2.refs_5_), channel_id=1, source_target_pairs={{0,1},{1,0},{2,3},{3,2},{4,5},{5,4},{6,7},{7,6},{8,9},{9,8},{10,11... | collective-permute-start | bytes 614408 | tf_op jit(solution)/shard_map/ppermute | solution.py:41
  18.7 0.0 collective-permute-done.4.refs_3_
  18.7 3.7 %shard_map.57 = (f32[4096,128]{1,0:T(8,128)S(1)}, f32[4096,256]{1,0:T(8,128)S(1)}) custom-call(bf16[4096,128]{1,0:T(8,128)(2,1)S(1)} %get-tuple-element.17.refs_0_, bf16[784,256]{1,0:T(8,128)(2,1)S(1)} %get-tuple-element.18.refs_1_, bf16[384,256]{1,0:T(8,128)(2,1)S(1)} %collective-permute-done.refs_2_, bf16[400,256]{1,0:T(8,128)(2,1)S(1)} %collective-permute-done.4.refs_3_, ...), custom_call_target="tpu_custom_call" | custom-call | flops 4026531840 | bytes 2097152 | tf_op jit(solution)/shard_map/pallas_call | solution.py:284
  22.4 1.3 %collective-permute-done.1.refs_2_ = bf16[384,256]{1,0:T(8,128)(2,1)S(1)} collective-permute-done((bf16[384,256]{1,0:T(8,128)(2,1)S(1)}, bf16[384,256]{1,0:T(8,128)(2,1)S(1)}, u32[]{:S(2)}, u32[]{:S(2)}) %collective-permute-start.1) | collective-permute-done | bytes 196640 | tf_op jit(solution)/shard_map/ppermute | solution.py:41
  23.8 0.7 %collective-permute-done.3.refs_3_ = bf16[400,256]{1,0:T(8,128)(2,1)S(1)} collective-permute-done((bf16[400,256]{1,0:T(8,128)(2,1)S(1)}, bf16[400,256]{1,0:T(8,128)(2,1)S(1)}, u32[]{:S(2)}, u32[]{:S(2)}) %collective-permute-start.3) | collective-permute-done | bytes 204832 | tf_op jit(solution)/shard_map/ppermute | solution.py:41
  24.5 1.3 %collective-permute-start.6 = (bf16[128,4096]{1,0:T(8,128)(2,1)S(1)}, bf16[128,4096]{1,0:T(8,128)(2,1)S(1)}, u32[]{:S(2)}, u32[]{:S(2)}) collective-permute-start(bf16[128,4096]{1,0:T(8,128)(2,1)S(1)} %shard_map.58), channel_id=1, source_target_pairs={{4,8},{12,16},{20,24},{28,0},{5,9},{13,17},{21,25},{29,1},{6,10},{... | collective-permute-start | bytes 3145736 | tf_op jit(solution)/shard_map/ppermute | solution.py:36
  25.8 2.0 %shard_map.59 = bf16[128,4096]{1,0:T(8,128)(2,1)S(1)} custom-call(bf16[4096,128]{1,0:T(8,128)(2,1)S(1)} %get-tuple-element.17.refs_0_, bf16[784,256]{1,0:T(8,128)(2,1)S(1)} %get-tuple-element.18.refs_1_, bf16[384,256]{1,0:T(8,128)(2,1)S(1)} %collective-permute-done.1.refs_2_, bf16[400,256]{1,0:T(8,128)(2,1)S(1)} %collective-permute-done.3.refs_3_, ...), custom_call_target="tpu_custom_call" | custom-call | flops 1610612736 | bytes 2097152 | tf_op jit(solution)/shard_map/pallas_call | solution.py:309
  27.8 2.9 %collective-permute-start.7 = (bf16[128,4096]{1,0:T(8,128)(2,1)S(1)}, bf16[128,4096]{1,0:T(8,128)(2,1)S(1)}, u32[]{:S(2)}, u32[]{:S(2)}) collective-permute-start(bf16[128,4096]{1,0:T(8,128)(2,1)S(1)} %shard_map.59), channel_id=1, source_target_pairs={{0,4},{8,12},{16,20},{24,28},{1,5},{9,13},{17,21},{25,29},{2,6},{1... | collective-permute-start | bytes 3145736 | tf_op jit(solution)/shard_map/ppermute | solution.py:36
  30.7 0.0 collective-permute-done.9.refs_1_
  30.7 1.7 %collective-permute-start.10 = (bf16[384,256]{1,0:T(8,128)(2,1)S(1)}, bf16[384,256]{1,0:T(8,128)(2,1)S(1)}, u32[]{:S(2)}, u32[]{:S(2)}) collective-permute-start(bf16[384,256]{1,0:T(8,128)(2,1)S(1)} %slice.20), channel_id=1, source_target_pairs={{0,1},{1,0},{2,3},{3,2},{4,5},{5,4},{6,7},{7,6},{8,9},{9,8},{10,11... | collective-permute-start | bytes 589832 | tf_op jit(solution)/shard_map/ppermute | solution.py:41
  32.4 1.5 %collective-permute-start.15 = (bf16[384,256]{1,0:T(8,128)(2,1)S(1)}, bf16[384,256]{1,0:T(8,128)(2,1)S(1)}, u32[]{:S(2)}, u32[]{:S(2)}) collective-permute-start(bf16[384,256]{1,0:T(8,128)(2,1)S(1)} %slice.20), channel_id=1, source_target_pairs={{0,2},{1,3},{2,0},{3,1},{4,6},{5,7},{6,4},{7,5},{8,10},{9,11},{10,... | collective-permute-start | bytes 589832 | tf_op jit(solution)/shard_map/ppermute | solution.py:41
  34.0 3.0 %collective-permute-done.10.refs_2_ = bf16[384,256]{1,0:T(8,128)(2,1)S(1)} collective-permute-done((bf16[384,256]{1,0:T(8,128)(2,1)S(1)}, bf16[384,256]{1,0:T(8,128)(2,1)S(1)}, u32[]{:S(2)}, u32[]{:S(2)}) %collective-permute-start.10) | collective-permute-done | bytes 196640 | tf_op jit(solution)/shard_map/ppermute | solution.py:41
  36.9 1.7 %collective-permute-start.12 = (bf16[400,256]{1,0:T(8,128)(2,1)S(1)}, bf16[400,256]{1,0:T(8,128)(2,1)S(1)}, u32[]{:S(2)}, u32[]{:S(2)}) collective-permute-start(bf16[400,256]{1,0:T(8,128)(2,1)S(1)} %slice.21), channel_id=1, source_target_pairs={{0,2},{1,3},{2,0},{3,1},{4,6},{5,7},{6,4},{7,5},{8,10},{9,11},{10,... | collective-permute-start | bytes 614408 | tf_op jit(solution)/shard_map/ppermute | solution.py:41
  38.6 0.0 collective-permute-done.15.refs_4_
  38.6 1.5 %collective-permute-start.14 = (bf16[400,256]{1,0:T(8,128)(2,1)S(1)}, bf16[400,256]{1,0:T(8,128)(2,1)S(1)}, u32[]{:S(2)}, u32[]{:S(2)}) collective-permute-start(bf16[400,256]{1,0:T(8,128)(2,1)S(1)} %slice.21), channel_id=1, source_target_pairs={{0,1},{1,0},{2,3},{3,2},{4,5},{5,4},{6,7},{7,6},{8,9},{9,8},{10,11... | collective-permute-start | bytes 614408 | tf_op jit(solution)/shard_map/ppermute | solution.py:41
  40.1 2.6 %collective-permute-done.12.refs_5_ = bf16[400,256]{1,0:T(8,128)(2,1)S(1)} collective-permute-done((bf16[400,256]{1,0:T(8,128)(2,1)S(1)}, bf16[400,256]{1,0:T(8,128)(2,1)S(1)}, u32[]{:S(2)}, u32[]{:S(2)}) %collective-permute-start.12) | collective-permute-done | bytes 204832 | tf_op jit(solution)/shard_map/ppermute | solution.py:41
  42.7 1.7 %collective-permute-start.11 = (bf16[384,256]{1,0:T(8,128)(2,1)S(1)}, bf16[384,256]{1,0:T(8,128)(2,1)S(1)}, u32[]{:S(2)}, u32[]{:S(2)}) collective-permute-start(bf16[384,256]{1,0:T(8,128)(2,1)S(1)} %collective-permute-done.10.refs_2_), channel_id=1, source_target_pairs={{0,2},{1,3},{2,0},{3,1},{4,6},{5,7},{6,4},{7,5},{8,10},{9,11},{10,... | collective-permute-start | bytes 589832 | tf_op jit(solution)/shard_map/ppermute | solution.py:41
  44.4 0.0 collective-permute-done.14.refs_3_
  44.4 1.6 %collective-permute-start.13 = (bf16[400,256]{1,0:T(8,128)(2,1)S(1)}, bf16[400,256]{1,0:T(8,128)(2,1)S(1)}, u32[]{:S(2)}, u32[]{:S(2)}) collective-permute-start(bf16[400,256]{1,0:T(8,128)(2,1)S(1)} %collective-permute-done.12.refs_5_), channel_id=1, source_target_pairs={{0,1},{1,0},{2,3},{3,2},{4,5},{5,4},{6,7},{7,6},{8,9},{9,8},{10,11... | collective-permute-start | bytes 614408 | tf_op jit(solution)/shard_map/ppermute | solution.py:41
  45.9 0.0 collective-permute-done.8.refs_0_
  45.9 3.7 %shard_map.60 = (f32[4096,128]{1,0:T(8,128)S(1)}, f32[4096,256]{1,0:T(8,128)S(1)}) custom-call(bf16[4096,128]{1,0:T(8,128)(2,1)S(1)} %collective-permute-done.8.refs_0_, bf16[784,256]{1,0:T(8,128)(2,1)S(1)} %collective-permute-done.9.refs_1_, bf16[384,256]{1,0:T(8,128)(2,1)S(1)} %collective-permute-done.10.refs_2_, ...), custom_call_target="tpu_custom_call" | custom-call | flops 4026531840 | bytes 2097152 | tf_op jit(solution)/shard_map/pallas_call | solution.py:284
  49.6 0.0 collective-permute-done.11.refs_2_
  49.6 0.5 collective-permute-done.13.refs_3_
  50.1 2.7 %shard_map.61.before = bf16[128,8192]{1,0:T(8,128)(2,1)} custom-call(bf16[4096,128]{1,0:T(8,128)(2,1)S(1)} %collective-permute-done.8.refs_0_, bf16[784,256]{1,0:T(8,128)(2,1)S(1)} %collective-permute-done.9.refs_1_, bf16[384,256]{1,0:T(8,128)(2,1)S(1)} %collective-permute-done.11.refs_2_, bf16[400,256]{1,0:T(8,128)(2,1)S(1)} %collective-permute-done.13.refs_3_, ...), custom_call_target="tpu_custom_call" | custom-call | flops 1610612736 | bytes 2097152 | tf_op jit(solution)/shard_map/pallas_call | solution.py:309
  52.8 0.0 collective-permute-done.6.from_odd
  52.8 0.0 collective-permute-done.7.from_even
  52.8 1.0 %shard_map.62 = bf16[128,8192]{1,0:T(8,128)(2,1)} custom-call(bf16[128,4096]{1,0:T(8,128)(2,1)S(1)} %collective-permute-done.6.from_odd, bf16[128,4096]{1,0:T(8,128)(2,1)S(1)} %collective-permute-done.7.from_even, bf16[128,8192]{1,0:T(8,128)(2,1)} %shard_map.61.before), custom_call_target="tpu_custom_call", output_to_operand_aliasing={{}: (2, {})} | custom-call | flops 1048576 | bytes 2097152 | tf_op jit(solution)/shard_map/pallas_call | solution.py:480
  (6 shorter events, 0.1 us)
Async XLA Ops:
  1.4 6.8 %copy-start = (bf16[1,128,8192]{2,1,0:T(8,128)(2,1)S(1)}, bf16[1,128,8192]{2,1,0:T(8,128)(2,1)}, u32[]{:S(2)}) copy-start(bf16[1,128,8192]{2,1,0:T(8,128)(2,1)} %param.5) | copy-start | bytes 6291460
  2.9 14.2 %collective-permute-start.2 = (bf16[400,256]{1,0:T(8,128)(2,1)S(1)}, bf16[400,256]{1,0:T(8,128)(2,1)S(1)}, u32[]{:S(2)}, u32[]{:S(2)}) collective-permute-start(bf16[400,256]{1,0:T(8,128)(2,1)S(1)} %slice.17), channel_id=1, source_target_pairs={{0,2},{1,3},{2,0},{3,1},{4,6},{5,7},{6,4},{7,5},{8,10},{9,11},{10,... | collective-permute-start | bytes 614408 | tf_op jit(solution)/shard_map/ppermute | solution.py:41
  6.0 12.8 %collective-permute-start.4 = (bf16[400,256]{1,0:T(8,128)(2,1)S(1)}, bf16[400,256]{1,0:T(8,128)(2,1)S(1)}, u32[]{:S(2)}, u32[]{:S(2)}) collective-permute-start(bf16[400,256]{1,0:T(8,128)(2,1)S(1)} %slice.17), channel_id=1, source_target_pairs={{0,1},{1,0},{2,3},{3,2},{4,5},{5,4},{6,7},{7,6},{8,9},{9,8},{10,11... | collective-permute-start | bytes 614408 | tf_op jit(solution)/shard_map/ppermute | solution.py:41
  7.5 9.2 %collective-permute-start = (bf16[384,256]{1,0:T(8,128)(2,1)S(1)}, bf16[384,256]{1,0:T(8,128)(2,1)S(1)}, u32[]{:S(2)}, u32[]{:S(2)}) collective-permute-start(bf16[384,256]{1,0:T(8,128)(2,1)S(1)} %slice.16), channel_id=1, source_target_pairs={{0,1},{1,0},{2,3},{3,2},{4,5},{5,4},{6,7},{7,6},{8,9},{9,8},{10,11... | collective-permute-start | bytes 589832 | tf_op jit(solution)/shard_map/ppermute | solution.py:41
  8.1 8.6 %collective-permute-start.5 = (bf16[384,256]{1,0:T(8,128)(2,1)S(1)}, bf16[384,256]{1,0:T(8,128)(2,1)S(1)}, u32[]{:S(2)}, u32[]{:S(2)}) collective-permute-start(bf16[384,256]{1,0:T(8,128)(2,1)S(1)} %slice.16), channel_id=1, source_target_pairs={{0,2},{1,3},{2,0},{3,1},{4,6},{5,7},{6,4},{7,5},{8,10},{9,11},{10,... | collective-permute-start | bytes 589832 | tf_op jit(solution)/shard_map/ppermute | solution.py:41
  9.2 36.7 %collective-permute-start.8 = (bf16[4096,128]{1,0:T(8,128)(2,1)S(1)}, bf16[4096,128]{1,0:T(8,128)(2,1)S(1)}, u32[]{:S(2)}, u32[]{:S(2)}) collective-permute-start(bf16[4096,128]{1,0:T(8,128)(2,1)S(1)} %get-tuple-element.21), channel_id=1, source_target_pairs={{0,4},{4,8},{8,12},{12,16},{16,20},{20,24},{24,28},{28,0},{1,5},{5... | collective-permute-start | bytes 3145736 | tf_op jit(solution)/shard_map/ppermute | solution.py:36
  16.7 14.0 %collective-permute-start.9 = (bf16[784,256]{1,0:T(8,128)(2,1)S(1)}, bf16[784,256]{1,0:T(8,128)(2,1)S(1)}, u32[]{:S(2)}, u32[]{:S(2)}) collective-permute-start(bf16[784,256]{1,0:T(8,128)(2,1)S(1)} %get-tuple-element.22), channel_id=1, source_target_pairs={{0,4},{4,8},{8,12},{12,16},{16,20},{20,24},{24,28},{28,0},{1,5},{5... | collective-permute-start | bytes 1204232 | tf_op jit(solution)/shard_map/ppermute | solution.py:36
  16.7 7.1 %collective-permute-start.1 = (bf16[384,256]{1,0:T(8,128)(2,1)S(1)}, bf16[384,256]{1,0:T(8,128)(2,1)S(1)}, u32[]{:S(2)}, u32[]{:S(2)}) collective-permute-start(bf16[384,256]{1,0:T(8,128)(2,1)S(1)} %collective-permute-done.refs_2_), channel_id=1, source_target_pairs={{0,2},{1,3},{2,0},{3,1},{4,6},{5,7},{6,4},{7,5},{8,10},{9,11},{10,... | collective-permute-start | bytes 589832 | tf_op jit(solution)/shard_map/ppermute | solution.py:41
  17.1 7.4 %collective-permute-start.3 = (bf16[400,256]{1,0:T(8,128)(2,1)S(1)}, bf16[400,256]{1,0:T(8,128)(2,1)S(1)}, u32[]{:S(2)}, u32[]{:S(2)}) collective-permute-start(bf16[400,256]{1,0:T(8,128)(2,1)S(1)} %collective-permute-done.2.refs_5_), channel_id=1, source_target_pairs={{0,1},{1,0},{2,3},{3,2},{4,5},{5,4},{6,7},{7,6},{8,9},{9,8},{10,11... | collective-permute-start | bytes 614408 | tf_op jit(solution)/shard_map/ppermute | solution.py:41
  24.5 28.3 %collective-permute-start.6 = (bf16[128,4096]{1,0:T(8,128)(2,1)S(1)}, bf16[128,4096]{1,0:T(8,128)(2,1)S(1)}, u32[]{:S(2)}, u32[]{:S(2)}) collective-permute-start(bf16[128,4096]{1,0:T(8,128)(2,1)S(1)} %shard_map.58), channel_id=1, source_target_pairs={{4,8},{12,16},{20,24},{28,0},{5,9},{13,17},{21,25},{29,1},{6,10},{... | collective-permute-start | bytes 3145736 | tf_op jit(solution)/shard_map/ppermute | solution.py:36
  27.8 25.1 %collective-permute-start.7 = (bf16[128,4096]{1,0:T(8,128)(2,1)S(1)}, bf16[128,4096]{1,0:T(8,128)(2,1)S(1)}, u32[]{:S(2)}, u32[]{:S(2)}) collective-permute-start(bf16[128,4096]{1,0:T(8,128)(2,1)S(1)} %shard_map.59), channel_id=1, source_target_pairs={{0,4},{8,12},{16,20},{24,28},{1,5},{9,13},{17,21},{25,29},{2,6},{1... | collective-permute-start | bytes 3145736 | tf_op jit(solution)/shard_map/ppermute | solution.py:36
  30.7 6.2 %collective-permute-start.10 = (bf16[384,256]{1,0:T(8,128)(2,1)S(1)}, bf16[384,256]{1,0:T(8,128)(2,1)S(1)}, u32[]{:S(2)}, u32[]{:S(2)}) collective-permute-start(bf16[384,256]{1,0:T(8,128)(2,1)S(1)} %slice.20), channel_id=1, source_target_pairs={{0,1},{1,0},{2,3},{3,2},{4,5},{5,4},{6,7},{7,6},{8,9},{9,8},{10,11... | collective-permute-start | bytes 589832 | tf_op jit(solution)/shard_map/ppermute | solution.py:41
  32.4 6.2 %collective-permute-start.15 = (bf16[384,256]{1,0:T(8,128)(2,1)S(1)}, bf16[384,256]{1,0:T(8,128)(2,1)S(1)}, u32[]{:S(2)}, u32[]{:S(2)}) collective-permute-start(bf16[384,256]{1,0:T(8,128)(2,1)S(1)} %slice.20), channel_id=1, source_target_pairs={{0,2},{1,3},{2,0},{3,1},{4,6},{5,7},{6,4},{7,5},{8,10},{9,11},{10,... | collective-permute-start | bytes 589832 | tf_op jit(solution)/shard_map/ppermute | solution.py:41
  36.9 5.8 %collective-permute-start.12 = (bf16[400,256]{1,0:T(8,128)(2,1)S(1)}, bf16[400,256]{1,0:T(8,128)(2,1)S(1)}, u32[]{:S(2)}, u32[]{:S(2)}) collective-permute-start(bf16[400,256]{1,0:T(8,128)(2,1)S(1)} %slice.21), channel_id=1, source_target_pairs={{0,2},{1,3},{2,0},{3,1},{4,6},{5,7},{6,4},{7,5},{8,10},{9,11},{10,... | collective-permute-start | bytes 614408 | tf_op jit(solution)/shard_map/ppermute | solution.py:41
  38.6 5.8 %collective-permute-start.14 = (bf16[400,256]{1,0:T(8,128)(2,1)S(1)}, bf16[400,256]{1,0:T(8,128)(2,1)S(1)}, u32[]{:S(2)}, u32[]{:S(2)}) collective-permute-start(bf16[400,256]{1,0:T(8,128)(2,1)S(1)} %slice.21), channel_id=1, source_target_pairs={{0,1},{1,0},{2,3},{3,2},{4,5},{5,4},{6,7},{7,6},{8,9},{9,8},{10,11... | collective-permute-start | bytes 614408 | tf_op jit(solution)/shard_map/ppermute | solution.py:41
  42.7 6.9 %collective-permute-start.11 = (bf16[384,256]{1,0:T(8,128)(2,1)S(1)}, bf16[384,256]{1,0:T(8,128)(2,1)S(1)}, u32[]{:S(2)}, u32[]{:S(2)}) collective-permute-start(bf16[384,256]{1,0:T(8,128)(2,1)S(1)} %collective-permute-done.10.refs_2_), channel_id=1, source_target_pairs={{0,2},{1,3},{2,0},{3,1},{4,6},{5,7},{6,4},{7,5},{8,10},{9,11},{10,... | collective-permute-start | bytes 589832 | tf_op jit(solution)/shard_map/ppermute | solution.py:41
  44.4 5.8 %collective-permute-start.13 = (bf16[400,256]{1,0:T(8,128)(2,1)S(1)}, bf16[400,256]{1,0:T(8,128)(2,1)S(1)}, u32[]{:S(2)}, u32[]{:S(2)}) collective-permute-start(bf16[400,256]{1,0:T(8,128)(2,1)S(1)} %collective-permute-done.12.refs_5_), channel_id=1, source_target_pairs={{0,1},{1,0},{2,3},{3,2},{4,5},{5,4},{6,7},{7,6},{8,9},{9,8},{10,11... | collective-permute-start | bytes 614408 | tf_op jit(solution)/shard_map/ppermute | solution.py:41

commit v3 on v2

--- a/solution.py
+++ b/solution.py
@@ -17,6 +17,7 @@
 
 ROPE_BASE = 500000.0
 MASKED = -1e30
+LENGTH_ROWS = 16
 FACTOR = math.log2(math.e) / math.sqrt(HEAD_SIZE)
 SPECS = (
     P("section", "sp", None),
@@ -26,14 +27,19 @@
     P("section"),
 )
 VMEM = pl.BlockSpec(memory_space=pltpu.VMEM)
+SMEM = pl.BlockSpec(memory_space=pltpu.SMEM)
 HBM = pl.BlockSpec(memory_space=pltpu.HBM)
 LIMIT = pltpu.CompilerParams(vmem_limit_bytes=20 * 2**20)
 
 
-def section_shift(value, side=None):
+def section_shift(value):
     count = lax.axis_size("section")
-    pairs = [(i, (i + 1) % count) for i in range(count) if side is None or i % 2 == side]
-    return lax.ppermute(value, "section", pairs)
+    return lax.ppermute(value, "section", [(i, (i + 1) % count) for i in range(count)])
+
+
+def section_swap(value):
+    count = lax.axis_size("section")
+    return lax.ppermute(value, "section", [(i, i ^ 1) for i in range(count)])
 
 
 def partner_swap(value, bits):
@@ -61,15 +67,12 @@
     return (wide * cosine + turned * sine).astype(jnp.bfloat16)
 
 
-def pack_kernel(
-    keyval, cache, offsets, lengths, frequency, *rest
-):
-    packs, (cosine, sine, loaded, offset, length, sem) = rest[:-6], rest[-6:]
+def pack_kernel(keyval, cache, frequency, offset, *rest):
+    packs, (cosine, sine, loaded, sem) = rest[:-4], rest[-4:]
     rows, positions = keyval.shape[0], cache.shape[1]
     heads = KEY_VALUE_HEADS // len(packs)
     middle = heads // 2 * rows
-    last = heads * rows + positions
-    moves = [(offsets, offset), (lengths, length), (keyval, loaded)]
+    moves = [(keyval, loaded)]
     for chunk, pack in enumerate(packs):
         moves.append((cache.at[chunk], pack.at[middle : middle + positions]))
     copies = [
@@ -78,7 +81,6 @@
     ]
     for copy in copies:
         copy.start()
-    copies[0].wait()
     first = offset[0] + lax.axis_index("sp") * rows
     place = first + lax.broadcasted_iota(jnp.int32, cosine.shape, 0)
     angle = place.astype(jnp.float32) * frequency[...]
@@ -86,10 +88,8 @@
     cosine[...] = jnp.cos(angle)
     turn = jnp.sin(angle)
     sine[...] = jnp.where(low, -turn, turn)
-    for copy in copies[1:]:
-        copy.wait()
+    copies[0].wait()
     cos_here, sin_here = cosine[...], sine[...]
-    live = length[0].astype(jnp.float32)
     for chunk, pack in enumerate(packs):
         for index in range(heads):
             start = index * rows + (positions if index >= heads // 2 else 0)
@@ -100,14 +100,18 @@
             pack[start : start + rows, HEAD_SIZE:] = loaded[
                 :, column + HEAD_SIZE : column + 2 * HEAD_SIZE
             ]
-        pack[last:, :] = jnp.full((pack.shape[0] - last, pack.shape[1]), live, jnp.float32).astype(
-            jnp.bfloat16
-        )
-
-
-def turn_kernel(query, cosine, sine, *turned):
+    for copy in copies[1:]:
+        copy.wait()
+
+
+def turn_kernel(query, cosine, sine, length, *turned):
     rows = query.shape[0]
     cos_here, sin_here = cosine[...], sine[...]
+    live = length[0].astype(jnp.float32)
+    for part in turned:
+        part[part.shape[0] - LENGTH_ROWS :, :] = jnp.full(
+            (LENGTH_ROWS, HEAD_SIZE), live, jnp.float32
+        ).astype(jnp.bfloat16)
     for head in range(QUERY_HEADS):
         pair = head // GROUP
         chunk, index = pair % len(turned), pair // len(turned)
@@ -131,11 +135,16 @@
     return jnp.dot(weights, values, preferred_element_type=jnp.float32)
 
 
-def live_mask(own, positions):
-    last = own.shape[0] - 16
-    length = own[last : last + 1, :].astype(jnp.float32)
+def own_heads(query, rows):
+    return (query.shape[0] - LENGTH_ROWS) // (GROUP * rows)
+
+
+def live_mask(query, positions):
+    last = query.shape[0] - LENGTH_ROWS
+    length = query[last : last + 1, :].astype(jnp.float32)
+    length = jnp.concatenate([length] * (positions // HEAD_SIZE), axis=1)
     place = lax.broadcasted_iota(jnp.int32, (1, positions), 1).astype(jnp.float32)
-    return place < length[:, :positions]
+    return place < length
 
 
 def run_on_side(body, side, *refs):
@@ -157,24 +166,20 @@
 def near_body(rows, query, own, *rest):
     halves, (top_ref, sums_ref, beside, above) = rest[:4], rest[4:]
     me = lax.axis_index("sp")
-    heads = query.shape[0] // (GROUP * rows)
-    positions = own.shape[0] - 16 - heads * rows
+    heads = own_heads(query, rows)
+    positions = own.shape[0] - heads * rows
     middle = heads // 2 * rows
     half = halves[0].shape[0]
     for block, first, second in ((beside, *halves[:2]), (above, *halves[2:])):
         block[:half, :] = first[...]
-        block[half:, :] = second[: block.shape[0] - half, :]
+        block[half:, :] = second[...]
     blocks = (own, beside, above)
-    live = live_mask(own, positions)
+    live = live_mask(query, positions)
     step_rows = STEP_HEADS * rows
-    causal = lax.broadcasted_iota(jnp.int32, (rows, rows), 1) <= lax.broadcasted_iota(
-        jnp.int32, (rows, rows), 0
-    )
-    causal = jnp.concatenate([causal] * STEP_HEADS, axis=0)
     for offset in range(len(blocks) + 1):
         head = me ^ offset
         start = pl.multiple_of(head * rows + jnp.where(head >= heads // 2, positions, 0), rows)
-        parts = [block[pl.ds(start, rows), :] for block in blocks]
+        parts = [block[pl.ds(start, rows), :] for block in blocks[1:]]
         if offset < len(blocks):
             parts.append(blocks[offset][middle : middle + positions, :])
         keys, values = stored_parts(parts)
@@ -182,12 +187,12 @@
         for step in range(GROUP // STEP_HEADS):
             place = pl.ds(base + step * step_rows, step_rows)
             scores = dot_scores(query[place, :], keys)
-            pieces = [jnp.where(causal, scores[:, :rows], MASKED)]
+            pieces = []
             for other in range(1, len(blocks)):
-                piece = scores[:, other * rows : (other + 1) * rows]
+                piece = scores[:, (other - 1) * rows : other * rows]
                 pieces.append(jnp.where((me ^ other) < me, piece, MASKED))
             if offset < len(blocks):
-                pieces.append(jnp.where(live, scores[:, len(blocks) * rows :], MASKED))
+                pieces.append(jnp.where(live, scores[:, (len(blocks) - 1) * rows :], MASKED))
             scores = jnp.concatenate(pieces, axis=1)
             top = jnp.max(scores, axis=1, keepdims=True)
             weights = jnp.exp2((scores - top) * FACTOR).astype(jnp.bfloat16)
@@ -202,21 +207,25 @@
 def far_body(rows, stride, query, own, first_half, second_half, top_ref, sums_ref, *rest):
     out, across, results, sem = rest if len(rest) == 4 else (*rest, None, None)
     me = lax.axis_index("sp")
-    heads = query.shape[0] // (GROUP * rows)
+    heads = own_heads(query, rows)
     half = first_half.shape[0]
     positions = 2 * half - heads * rows
     middle = heads // 2 * rows
     width = GROUP * HEAD_SIZE
     across[:half, :] = first_half[...]
-    across[half:, :] = second_half[: across.shape[0] - half, :]
-    live = live_mask(own, positions)
+    across[half:, :] = second_half[...]
+    live = live_mask(query, positions)
     step_rows = STEP_HEADS * rows
+    causal = lax.broadcasted_iota(jnp.int32, (rows, rows), 1) <= lax.broadcasted_iota(
+        jnp.int32, (rows, rows), 0
+    )
+    causal = jnp.concatenate([causal] * STEP_HEADS, axis=0)
     far = heads - 1
     copies = []
     for offset in range(heads):
         head = me ^ offset
         start = pl.multiple_of(head * rows + jnp.where(head >= heads // 2, positions, 0), rows)
-        parts = [across[pl.ds(start, rows), :]]
+        parts = [own[pl.ds(start, rows), :], across[pl.ds(start, rows), :]]
         if offset == far:
             parts.append(across[middle : middle + positions, :])
         keys, values = stored_parts(parts)
@@ -224,9 +233,12 @@
         for step in range(GROUP // STEP_HEADS):
             place = pl.ds(base + step * step_rows, step_rows)
             scores = dot_scores(query[place, :], keys)
-            pieces = [jnp.where((me ^ far) < me, scores[:, :rows], MASKED)]
+            pieces = [
+                jnp.where(causal, scores[:, :rows], MASKED),
+                jnp.where((me ^ far) < me, scores[:, rows : 2 * rows], MASKED),
+            ]
             if offset == far:
-                pieces.append(jnp.where(live, scores[:, rows:], MASKED))
+                pieces.append(jnp.where(live, scores[:, 2 * rows :], MASKED))
             scores = jnp.concatenate(pieces, axis=1)
             before = top_ref[place, :]
             top = jnp.maximum(jnp.max(scores, axis=1, keepdims=True), before)
@@ -279,13 +291,13 @@
 
 
 def near(turned, rows, own, beside, above, side=None):
-    block = pltpu.VMEM((own.shape[0] - 16, own.shape[1]), jnp.bfloat16)
+    block = pltpu.VMEM(own.shape, jnp.bfloat16)
     work = turned.shape[0] * 5 * rows
     return pl.pallas_call(
         functools.partial(near_kernel, rows, side),
         out_shape=[
-            pltpu.VMEM((turned.shape[0], HEAD_SIZE), jnp.float32),
-            pltpu.VMEM((turned.shape[0], 2 * HEAD_SIZE), jnp.float32),
+            pltpu.VMEM((turned.shape[0] - LENGTH_ROWS, HEAD_SIZE), jnp.float32),
+            pltpu.VMEM((turned.shape[0] - LENGTH_ROWS, 2 * HEAD_SIZE), jnp.float32),
         ],
         in_specs=[VMEM] * 6,
         out_specs=[VMEM] * 2,
@@ -299,7 +311,7 @@
 
 def far(turned, rows, own, first_half, second_half, state, stride=1, side=None):
     work = turned.shape[0] * 2 * rows
-    width = turned.shape[0] // rows * HEAD_SIZE
+    width = (turned.shape[0] - LENGTH_ROWS) // rows * HEAD_SIZE
     heads = width // (GROUP * HEAD_SIZE)
     scratch = [pltpu.VMEM((2 * first_half.shape[0], 2 * HEAD_SIZE), jnp.bfloat16)]
     if stride > 1:
@@ -429,33 +441,32 @@
     chunks = cache.shape[1]
     heads = KEY_VALUE_HEADS // chunks
     half = (heads * rows + cache.shape[2]) // 2
-    pack = pltpu.VMEM((2 * half + 16, 2 * HEAD_SIZE), jnp.bfloat16)
+    pack = pltpu.VMEM((2 * half, 2 * HEAD_SIZE), jnp.bfloat16)
     table = pltpu.VMEM((rows, HEAD_SIZE), jnp.float32)
     items = [pltpu.with_memory_space_constraint(x, pltpu.HBM) for x in (keyval[0], cache[0])]
-    items += [offsets, lengths]
     here, ahead, cosine, sine = pl.pallas_call(
         pack_kernel,
         out_shape=[pack] * chunks + [table] * 2,
-        in_specs=[HBM] * 4 + [VMEM],
+        in_specs=[HBM] * 2 + [VMEM, SMEM],
         out_specs=[VMEM] * (chunks + 2),
         scratch_shapes=[
             pltpu.VMEM(keyval.shape[1:], jnp.bfloat16),
-            pltpu.SMEM((1,), jnp.int32),
-            pltpu.SMEM((1,), jnp.int32),
-            pltpu.SemaphoreType.DMA((3 + chunks,)),
+            pltpu.SemaphoreType.DMA((1 + chunks,)),
         ],
         compiler_params=LIMIT,
         cost_estimate=pl.CostEstimate(flops=2**30, bytes_accessed=2**21, transcendentals=0),
-    )(*items, rotation_frequency(HEAD_SIZE)[None])
-    turned = pltpu.VMEM((query.size // (HEAD_SIZE * chunks), HEAD_SIZE), jnp.bfloat16)
+    )(*items, rotation_frequency(HEAD_SIZE)[None], offsets)
+    lengths, cosine = lax.optimization_barrier((lengths, cosine))
+    turned_rows = query.size // (HEAD_SIZE * chunks) + LENGTH_ROWS
+    turned = pltpu.VMEM((turned_rows, HEAD_SIZE), jnp.bfloat16)
     turned_here, turned_ahead = pl.pallas_call(
         turn_kernel,
         out_shape=[turned] * chunks,
-        in_specs=[VMEM] * 3,
+        in_specs=[VMEM] * 3 + [SMEM],
         out_specs=[VMEM] * chunks,
         compiler_params=LIMIT,
         cost_estimate=pl.CostEstimate(flops=2**30, bytes_accessed=2**23, transcendentals=0),
-    )(query[0], cosine, sine)
+    )(query[0], cosine, sine, lengths)
     beside = [partner_swap(here[:half], 1)]
     above = [partner_swap(here[half:], 2)]
     beside.append(partner_swap(here[half:], 1))
@@ -469,10 +480,10 @@
     moved_beside.append(partner_swap(moved_pack[half:], 1))
     moved_above.insert(0, partner_swap(moved_pack[:half], 2))
     state = near(turned_here, rows, here, beside, above)
-    passed = []
-    for side in (1, 0):
-        attended = far(turned_here, rows, here, first_half, second_half, state, side=side)
-        passed.append(section_shift(attended, side))
+    attended = far(turned_here, rows, here, first_half, second_half, state, side=1)
+    from_odd = section_shift(attended)
+    attended = far(turned_here, rows, here, first_half, second_half, state, side=0)
+    from_even = section_swap(attended)
     moved_first = partner_swap(moved_beside[0], 2)
     moved_second = partner_swap(moved_above[1], 1)
     state = near(moved_query, rows, moved_pack, moved_beside, moved_above)
@@ -486,7 +497,7 @@
         input_output_aliases={2: 0},
         compiler_params=LIMIT,
         cost_estimate=pl.CostEstimate(flops=2**20, bytes_accessed=2**21, transcendentals=0),
-    )(*passed, out)
+    )(from_odd, from_even, out)
     return out[None]
 
 

time: 54.2 us -> 54.8 us (1.011)
  Pallas kernels: 15.6 us -> 14.4 us
  waiting for transfers between devices: 15.6 us -> 16.6 us
  starting transfers between devices: 21.1 us -> 21.9 us
    ppermute x4, waiting for transfers between devices: 0.01 us -> 3.5 us  [the longest x3 3.5 us: section_shift(): lax.ppermute(value, 'section', [(i, (i + 1) % count) for i in range(count)])]
    ppermute x12, starting transfers between devices: 16.9 us -> 19.8 us  [partner_swap(): return lax.ppermute(value, 'sp', [(i, i ^ bits) for i in range(count)])]
    pallas_call x2, Pallas kernels: 7.35 us -> 4.77 us  [near(): pl.pallas_call(functools.partial(near_kernel, rows, side), out_shape=[plt...]
    ppermute x12, waiting for transfers between devices: 15.5 us -> 13.1 us  [partner_swap(): return lax.ppermute(value, 'sp', [(i, i ^ bits) for i in range(count)])]
    ppermute x4, starting transfers between devices: 4.28 us -> 2.13 us  [the longest x3 2.06 us: section_shift(): lax.ppermute(value, 'section', [(i, (i + 1) % count) for i in range(count)])]
    pallas_call x3, Pallas kernels: 4.68 us -> 6.12 us  [far(): pl.pallas_call(functools.partial(far_kernel, rows, stride, side), out_sha...]
  transfers between devices with their start and end apart: 16 -> 16, of which waited for: 6 -> 10; matrix products, arithmetic and copies ran while one was open for 0% -> 0% of each run, Pallas kernels for 24% -> 22%
where the time goes in v3:
time: 54.8 us; the launch traced here: 54.6 us
  starting transfers between devices  21.9 us (40%)
  waiting for transfers between devices  16.6 us (30%)
  Pallas kernels  14.4 us (26%)
  between operations  1.59 us (3%)
    ppermute x12, starting transfers between devices, partner_swap(): return lax.ppermute(value, 'sp', [(i, i ^ bits) for i in range(count)])  19.8 us
    ppermute x12, waiting for transfers between devices, partner_swap(): return lax.ppermute(value, 'sp', [(i, i ^ bits) for i in range(count)])  13.1 us
    pallas_call x3, Pallas kernels, far(): pl.pallas_call(functools.partial(far_kernel, rows, stride, side), out_sha...  6.12 us
    pallas_call x2, Pallas kernels, near(): pl.pallas_call(functools.partial(near_kernel, rows, side), out_shape=[plt...  4.77 us
    ppermute x3, waiting for transfers between devices, section_shift(): lax.ppermute(value, 'section', [(i, (i + 1) % count) for i in range(count)])  3.5 us
    ppermute x3, starting transfers between devices, section_shift(): lax.ppermute(value, 'section', [(i, (i + 1) % count) for i in range(count)])  2.06 us
    pallas_call x1, Pallas kernels, on_device(): pl.pallas_call(pack_kernel, out_shape=[pack] * chunks + [table] * 2, in_s...  1.42 us
  transfers between devices with their start and end apart: 16, of which 10 were waited for; matrix products, arithmetic and copies ran while one was open for 0% of the time, Pallas kernels for 22%

profile of v3, /device:TPU:0, one launch (start us, length us, event | category | flops | bytes accessed | tf_op | source)
XLA Modules:
  0.0 54.6 jit_solution(14012870626328358582)
XLA Ops:
  0.0 0.1 maximum_bitcast_fusion.frequency
  0.7 0.0 copy-start
  0.8 1.4 %shard_map.55 = (bf16[768,256]{1,0:T(8,128)(2,1)S(1)}, bf16[768,256]{1,0:T(8,128)(2,1)S(1)}, f32[128,128]{1,0:T(8,128)S(1)}, f32[128,128]{1,0:T(8,128)S(1)}) custom-call(bf16[128,2048]{1,0:T(8,128)(2,1)} %bitcast.7, bf16[2,256,256]{2,1,0:T(8,128)(2,1)} %bitcast.8, f32[1,128]{1,0:T(1,128)S(1)} %maximum_bitcast_fusion.frequency, s32[1]{0:T(128)S(6)} %copy.8.offset), custom_call_target="tpu_custom_call" | custom-call | flops 1073741824 | bytes 2097152 | tf_op jit(solution)/shard_map/pallas_call | solution.py:447
  2.2 3.0 %collective-permute-start = (bf16[384,256]{1,0:T(8,128)(2,1)S(1)}, bf16[384,256]{1,0:T(8,128)(2,1)S(1)}, u32[]{:S(2)}, u32[]{:S(2)}) collective-permute-start(bf16[384,256]{1,0:T(8,128)(2,1)S(1)} %get-tuple-element.32), channel_id=1, source_target_pairs={{0,1},{1,0},{2,3},{3,2},{4,5},{5,4},{6,7},{7,6},{8,9},{9,8},{10,11... | collective-permute-start | bytes 589832 | tf_op jit(solution)/shard_map/ppermute | solution.py:47
  5.3 1.5 %collective-permute-start.2 = (bf16[384,256]{1,0:T(8,128)(2,1)S(1)}, bf16[384,256]{1,0:T(8,128)(2,1)S(1)}, u32[]{:S(2)}, u32[]{:S(2)}) collective-permute-start(bf16[384,256]{1,0:T(8,128)(2,1)S(1)} %get-tuple-element.31), channel_id=1, source_target_pairs={{0,2},{1,3},{2,0},{3,1},{4,6},{5,7},{6,4},{7,5},{8,10},{9,11},{10,... | collective-permute-start | bytes 589832 | tf_op jit(solution)/shard_map/ppermute | solution.py:47
  6.8 0.5 collective-permute-start.4
  7.3 0.1 collective-permute-start.5
  8.0 0.0 copy-done
  8.0 1.0 %shard_map.56 = (bf16[4112,128]{1,0:T(8,128)(2,1)S(1)}, bf16[4112,128]{1,0:T(8,128)(2,1)S(1)}) custom-call(bf16[128,8192]{1,0:T(8,128)(2,1)S(1)} %bitcast.6, f32[128,128]{1,0:T(8,128)S(1)} %get-tuple-element.18.cosine, f32[128,128]{1,0:T(8,128)S(1)} %get-tuple-element.19.sine, s32[1]{0:T(128)S(6)} %copy.9.length), custom_call_target="tpu_custom_call" | custom-call | flops 1073741824 | bytes 8388608 | tf_op jit(solution)/shard_map/pallas_call | solution.py:462
  9.1 0.1 collective-permute-start.8
  9.1 1.9 %collective-permute-done.refs_2_ = bf16[384,256]{1,0:T(8,128)(2,1)S(1)} collective-permute-done((bf16[384,256]{1,0:T(8,128)(2,1)S(1)}, bf16[384,256]{1,0:T(8,128)(2,1)S(1)}, u32[]{:S(2)}, u32[]{:S(2)}) %collective-permute-start) | collective-permute-done | bytes 196640 | tf_op jit(solution)/shard_map/ppermute | solution.py:47
  11.0 0.3 collective-permute-start.9
  11.3 1.8 %collective-permute-done.2.refs_5_ = bf16[384,256]{1,0:T(8,128)(2,1)S(1)} collective-permute-done((bf16[384,256]{1,0:T(8,128)(2,1)S(1)}, bf16[384,256]{1,0:T(8,128)(2,1)S(1)}, u32[]{:S(2)}, u32[]{:S(2)}) %collective-permute-start.2) | collective-permute-done | bytes 196640 | tf_op jit(solution)/shard_map/ppermute | solution.py:47
  13.0 1.5 %collective-permute-start.1 = (bf16[384,256]{1,0:T(8,128)(2,1)S(1)}, bf16[384,256]{1,0:T(8,128)(2,1)S(1)}, u32[]{:S(2)}, u32[]{:S(2)}) collective-permute-start(bf16[384,256]{1,0:T(8,128)(2,1)S(1)} %collective-permute-done.refs_2_), channel_id=1, source_target_pairs={{0,2},{1,3},{2,0},{3,1},{4,6},{5,7},{6,4},{7,5},{8,10},{9,11},{10,... | collective-permute-start | bytes 589832 | tf_op jit(solution)/shard_map/ppermute | solution.py:47
  14.5 0.0 collective-permute-done.4.refs_3_
  14.5 1.6 %collective-permute-start.3 = (bf16[384,256]{1,0:T(8,128)(2,1)S(1)}, bf16[384,256]{1,0:T(8,128)(2,1)S(1)}, u32[]{:S(2)}, u32[]{:S(2)}) collective-permute-start(bf16[384,256]{1,0:T(8,128)(2,1)S(1)} %collective-permute-done.2.refs_5_), channel_id=1, source_target_pairs={{0,1},{1,0},{2,3},{3,2},{4,5},{5,4},{6,7},{7,6},{8,9},{9,8},{10,11... | collective-permute-start | bytes 589832 | tf_op jit(solution)/shard_map/ppermute | solution.py:47
  16.1 0.0 collective-permute-done.5.refs_4_
  16.1 2.4 %shard_map.57 = (f32[4096,128]{1,0:T(8,128)S(1)}, f32[4096,256]{1,0:T(8,128)S(1)}) custom-call(bf16[4112,128]{1,0:T(8,128)(2,1)S(1)} %get-tuple-element.21.refs_0_, bf16[768,256]{1,0:T(8,128)(2,1)S(1)} %get-tuple-element.22.refs_1_, bf16[384,256]{1,0:T(8,128)(2,1)S(1)} %collective-permute-done.refs_2_, bf16[384,256]{1,0:T(8,128)(2,1)S(1)} %collective-permute-done.4.refs_3_, ...), custom_call_target="tpu_custom_call" | custom-call | flops 4042260480 | bytes 2105344 | tf_op jit(solution)/shard_map/pallas_call | solution.py:296
  18.5 1.5 %collective-permute-done.1.refs_2_ = bf16[384,256]{1,0:T(8,128)(2,1)S(1)} collective-permute-done((bf16[384,256]{1,0:T(8,128)(2,1)S(1)}, bf16[384,256]{1,0:T(8,128)(2,1)S(1)}, u32[]{:S(2)}, u32[]{:S(2)}) %collective-permute-start.1) | collective-permute-done | bytes 196640 | tf_op jit(solution)/shard_map/ppermute | solution.py:47
  20.0 1.2 %collective-permute-done.3.refs_3_ = bf16[384,256]{1,0:T(8,128)(2,1)S(1)} collective-permute-done((bf16[384,256]{1,0:T(8,128)(2,1)S(1)}, bf16[384,256]{1,0:T(8,128)(2,1)S(1)}, u32[]{:S(2)}, u32[]{:S(2)}) %collective-permute-start.3) | collective-permute-done | bytes 196640 | tf_op jit(solution)/shard_map/ppermute | solution.py:47
  21.3 1.7 %collective-permute-start.6 = (bf16[128,4096]{1,0:T(8,128)(2,1)S(1)}, bf16[128,4096]{1,0:T(8,128)(2,1)S(1)}, u32[]{:S(2)}, u32[]{:S(2)}) collective-permute-start(bf16[128,4096]{1,0:T(8,128)(2,1)S(1)} %shard_map.58), channel_id=1, source_target_pairs={{0,4},{4,8},{8,12},{12,16},{16,20},{20,24},{24,28},{28,0},{1,5},{5... | collective-permute-start | bytes 3145736 | tf_op jit(solution)/shard_map/ppermute | solution.py:37
  23.0 2.8 %shard_map.59 = bf16[128,4096]{1,0:T(8,128)(2,1)S(1)} custom-call(bf16[4112,128]{1,0:T(8,128)(2,1)S(1)} %get-tuple-element.21.refs_0_, bf16[768,256]{1,0:T(8,128)(2,1)S(1)} %get-tuple-element.22.refs_1_, bf16[384,256]{1,0:T(8,128)(2,1)S(1)} %collective-permute-done.1.refs_2_, bf16[384,256]{1,0:T(8,128)(2,1)S(1)} %collective-permute-done.3.refs_3_, ...), custom_call_target="tpu_custom_call" | custom-call | flops 1616904192 | bytes 2105344 | tf_op jit(solution)/shard_map/pallas_call | solution.py:321
  25.8 0.1 collective-permute-start.7
  25.9 3.5 %collective-permute-done.9.refs_1_ = bf16[768,256]{1,0:T(8,128)(2,1)S(1)} collective-permute-done((bf16[768,256]{1,0:T(8,128)(2,1)S(1)}, bf16[768,256]{1,0:T(8,128)(2,1)S(1)}, u32[]{:S(2)}, u32[]{:S(2)}) %collective-permute-start.9) | collective-permute-done | bytes 393248 | tf_op jit(solution)/shard_map/ppermute | solution.py:37
  29.4 2.0 %collective-permute-start.10 = (bf16[384,256]{1,0:T(8,128)(2,1)S(1)}, bf16[384,256]{1,0:T(8,128)(2,1)S(1)}, u32[]{:S(2)}, u32[]{:S(2)}) collective-permute-start(bf16[384,256]{1,0:T(8,128)(2,1)S(1)} %get-tuple-element.30), channel_id=1, source_target_pairs={{0,1},{1,0},{2,3},{3,2},{4,5},{5,4},{6,7},{7,6},{8,9},{9,8},{10,11... | collective-permute-start | bytes 589832 | tf_op jit(solution)/shard_map/ppermute | solution.py:47
  31.4 1.5 %collective-permute-start.12 = (bf16[384,256]{1,0:T(8,128)(2,1)S(1)}, bf16[384,256]{1,0:T(8,128)(2,1)S(1)}, u32[]{:S(2)}, u32[]{:S(2)}) collective-permute-start(bf16[384,256]{1,0:T(8,128)(2,1)S(1)} %get-tuple-element.29), channel_id=1, source_target_pairs={{0,2},{1,3},{2,0},{3,1},{4,6},{5,7},{6,4},{7,5},{8,10},{9,11},{10,... | collective-permute-start | bytes 589832 | tf_op jit(solution)/shard_map/ppermute | solution.py:47
  33.0 2.6 %collective-permute-done.10.refs_2_ = bf16[384,256]{1,0:T(8,128)(2,1)S(1)} collective-permute-done((bf16[384,256]{1,0:T(8,128)(2,1)S(1)}, bf16[384,256]{1,0:T(8,128)(2,1)S(1)}, u32[]{:S(2)}, u32[]{:S(2)}) %collective-permute-start.10) | collective-permute-done | bytes 196640 | tf_op jit(solution)/shard_map/ppermute | solution.py:47
  35.5 2.4 %collective-permute-start.14 = (bf16[384,256]{1,0:T(8,128)(2,1)S(1)}, bf16[384,256]{1,0:T(8,128)(2,1)S(1)}, u32[]{:S(2)}, u32[]{:S(2)}) collective-permute-start(bf16[384,256]{1,0:T(8,128)(2,1)S(1)} %get-tuple-element.29), channel_id=1, source_target_pairs={{0,1},{1,0},{2,3},{3,2},{4,5},{5,4},{6,7},{7,6},{8,9},{9,8},{10,11... | collective-permute-start | bytes 589832 | tf_op jit(solution)/shard_map/ppermute | solution.py:47
  38.0 0.3 collective-permute-done.12.refs_5_
  38.2 1.5 %collective-permute-start.15 = (bf16[384,256]{1,0:T(8,128)(2,1)S(1)}, bf16[384,256]{1,0:T(8,128)(2,1)S(1)}, u32[]{:S(2)}, u32[]{:S(2)}) collective-permute-start(bf16[384,256]{1,0:T(8,128)(2,1)S(1)} %get-tuple-element.30), channel_id=1, source_target_pairs={{0,2},{1,3},{2,0},{3,1},{4,6},{5,7},{6,4},{7,5},{8,10},{9,11},{10,... | collective-permute-start | bytes 589832 | tf_op jit(solution)/shard_map/ppermute | solution.py:47
  39.7 1.9 %collective-permute-done.14.refs_3_ = bf16[384,256]{1,0:T(8,128)(2,1)S(1)} collective-permute-done((bf16[384,256]{1,0:T(8,128)(2,1)S(1)}, bf16[384,256]{1,0:T(8,128)(2,1)S(1)}, u32[]{:S(2)}, u32[]{:S(2)}) %collective-permute-start.14) | collective-permute-done | bytes 196640 | tf_op jit(solution)/shard_map/ppermute | solution.py:47
  41.6 2.3 %collective-permute-start.11 = (bf16[384,256]{1,0:T(8,128)(2,1)S(1)}, bf16[384,256]{1,0:T(8,128)(2,1)S(1)}, u32[]{:S(2)}, u32[]{:S(2)}) collective-permute-start(bf16[384,256]{1,0:T(8,128)(2,1)S(1)} %collective-permute-done.10.refs_2_), channel_id=1, source_target_pairs={{0,2},{1,3},{2,0},{3,1},{4,6},{5,7},{6,4},{7,5},{8,10},{9,11},{10,... | collective-permute-start | bytes 589832 | tf_op jit(solution)/shard_map/ppermute | solution.py:47
  43.9 0.6 %collective-permute-done.15.refs_4_ = bf16[384,256]{1,0:T(8,128)(2,1)S(1)} collective-permute-done((bf16[384,256]{1,0:T(8,128)(2,1)S(1)}, bf16[384,256]{1,0:T(8,128)(2,1)S(1)}, u32[]{:S(2)}, u32[]{:S(2)}) %collective-permute-start.15) | collective-permute-done | bytes 196640 | tf_op jit(solution)/shard_map/ppermute | solution.py:47
  44.4 1.9 %collective-permute-start.13 = (bf16[384,256]{1,0:T(8,128)(2,1)S(1)}, bf16[384,256]{1,0:T(8,128)(2,1)S(1)}, u32[]{:S(2)}, u32[]{:S(2)}) collective-permute-start(bf16[384,256]{1,0:T(8,128)(2,1)S(1)} %collective-permute-done.12.refs_5_), channel_id=1, source_target_pairs={{0,1},{1,0},{2,3},{3,2},{4,5},{5,4},{6,7},{7,6},{8,9},{9,8},{10,11... | collective-permute-start | bytes 589832 | tf_op jit(solution)/shard_map/ppermute | solution.py:47
  46.3 0.0 collective-permute-done.8.refs_0_
  46.3 2.4 %shard_map.60 = (f32[4096,128]{1,0:T(8,128)S(1)}, f32[4096,256]{1,0:T(8,128)S(1)}) custom-call(bf16[4112,128]{1,0:T(8,128)(2,1)S(1)} %collective-permute-done.8.refs_0_, bf16[768,256]{1,0:T(8,128)(2,1)S(1)} %collective-permute-done.9.refs_1_, bf16[384,256]{1,0:T(8,128)(2,1)S(1)} %collective-permute-done.10.refs_2_, ...), custom_call_target="tpu_custom_call" | custom-call | flops 4042260480 | bytes 2105344 | tf_op jit(solution)/shard_map/pallas_call | solution.py:296
  48.7 0.0 collective-permute-done.11.refs_2_
  48.7 1.4 %collective-permute-done.13.refs_3_ = bf16[384,256]{1,0:T(8,128)(2,1)S(1)} collective-permute-done((bf16[384,256]{1,0:T(8,128)(2,1)S(1)}, bf16[384,256]{1,0:T(8,128)(2,1)S(1)}, u32[]{:S(2)}, u32[]{:S(2)}) %collective-permute-start.13) | collective-permute-done | bytes 196640 | tf_op jit(solution)/shard_map/ppermute | solution.py:47
  50.1 3.3 %shard_map.61.before = bf16[128,8192]{1,0:T(8,128)(2,1)} custom-call(bf16[4112,128]{1,0:T(8,128)(2,1)S(1)} %collective-permute-done.8.refs_0_, bf16[768,256]{1,0:T(8,128)(2,1)S(1)} %collective-permute-done.9.refs_1_, bf16[384,256]{1,0:T(8,128)(2,1)S(1)} %collective-permute-done.11.refs_2_, bf16[384,256]{1,0:T(8,128)(2,1)S(1)} %collective-permute-done.13.refs_3_, ...), custom_call_target="tpu_custom_call" | custom-call | flops 1616904192 | bytes 2105344 | tf_op jit(solution)/shard_map/pallas_call | solution.py:321
  53.4 0.0 collective-permute-done.6.from_odd
  53.4 0.0 collective-permute-done.7.from_even
  53.5 1.0 %shard_map.62 = bf16[128,8192]{1,0:T(8,128)(2,1)} custom-call(bf16[128,4096]{1,0:T(8,128)(2,1)S(1)} %collective-permute-done.6.from_odd, bf16[128,4096]{1,0:T(8,128)(2,1)S(1)} %collective-permute-done.7.from_even, bf16[128,8192]{1,0:T(8,128)(2,1)} %shard_map.61.before), custom_call_target="tpu_custom_call", output_to_operand_aliasing={{}: (2, {})} | custom-call | flops 1048576 | bytes 2097152 | tf_op jit(solution)/shard_map/pallas_call | solution.py:491
  (4 shorter events, 0.1 us)
Async XLA Ops:
  0.7 7.3 %copy-start = (bf16[1,128,8192]{2,1,0:T(8,128)(2,1)S(1)}, bf16[1,128,8192]{2,1,0:T(8,128)(2,1)}, u32[]{:S(2)}) copy-start(bf16[1,128,8192]{2,1,0:T(8,128)(2,1)} %param.5) | copy-start | bytes 6291460
  2.2 8.8 %collective-permute-start = (bf16[384,256]{1,0:T(8,128)(2,1)S(1)}, bf16[384,256]{1,0:T(8,128)(2,1)S(1)}, u32[]{:S(2)}, u32[]{:S(2)}) collective-permute-start(bf16[384,256]{1,0:T(8,128)(2,1)S(1)} %get-tuple-element.32), channel_id=1, source_target_pairs={{0,1},{1,0},{2,3},{3,2},{4,5},{5,4},{6,7},{7,6},{8,9},{9,8},{10,11... | collective-permute-start | bytes 589832 | tf_op jit(solution)/shard_map/ppermute | solution.py:47
  5.3 7.8 %collective-permute-start.2 = (bf16[384,256]{1,0:T(8,128)(2,1)S(1)}, bf16[384,256]{1,0:T(8,128)(2,1)S(1)}, u32[]{:S(2)}, u32[]{:S(2)}) collective-permute-start(bf16[384,256]{1,0:T(8,128)(2,1)S(1)} %get-tuple-element.31), channel_id=1, source_target_pairs={{0,2},{1,3},{2,0},{3,1},{4,6},{5,7},{6,4},{7,5},{8,10},{9,11},{10,... | collective-permute-start | bytes 589832 | tf_op jit(solution)/shard_map/ppermute | solution.py:47
  6.8 7.8 %collective-permute-start.4 = (bf16[384,256]{1,0:T(8,128)(2,1)S(1)}, bf16[384,256]{1,0:T(8,128)(2,1)S(1)}, u32[]{:S(2)}, u32[]{:S(2)}) collective-permute-start(bf16[384,256]{1,0:T(8,128)(2,1)S(1)} %get-tuple-element.31), channel_id=1, source_target_pairs={{0,1},{1,0},{2,3},{3,2},{4,5},{5,4},{6,7},{7,6},{8,9},{9,8},{10,11... | collective-permute-start | bytes 589832 | tf_op jit(solution)/shard_map/ppermute | solution.py:47
  7.3 8.8 %collective-permute-start.5 = (bf16[384,256]{1,0:T(8,128)(2,1)S(1)}, bf16[384,256]{1,0:T(8,128)(2,1)S(1)}, u32[]{:S(2)}, u32[]{:S(2)}) collective-permute-start(bf16[384,256]{1,0:T(8,128)(2,1)S(1)} %get-tuple-element.32), channel_id=1, source_target_pairs={{0,2},{1,3},{2,0},{3,1},{4,6},{5,7},{6,4},{7,5},{8,10},{9,11},{10,... | collective-permute-start | bytes 589832 | tf_op jit(solution)/shard_map/ppermute | solution.py:47
  9.1 37.2 %collective-permute-start.8 = (bf16[4112,128]{1,0:T(8,128)(2,1)S(1)}, bf16[4112,128]{1,0:T(8,128)(2,1)S(1)}, u32[]{:S(2)}, u32[]{:S(2)}) collective-permute-start(bf16[4112,128]{1,0:T(8,128)(2,1)S(1)} %get-tuple-element.25), channel_id=1, source_target_pairs={{0,4},{4,8},{8,12},{12,16},{16,20},{20,24},{24,28},{28,0},{1,5},{5... | collective-permute-start | bytes 3158024 | tf_op jit(solution)/shard_map/ppermute | solution.py:37
  11.0 18.4 %collective-permute-start.9 = (bf16[768,256]{1,0:T(8,128)(2,1)S(1)}, bf16[768,256]{1,0:T(8,128)(2,1)S(1)}, u32[]{:S(2)}, u32[]{:S(2)}) collective-permute-start(bf16[768,256]{1,0:T(8,128)(2,1)S(1)} %get-tuple-element.26), channel_id=1, source_target_pairs={{0,4},{4,8},{8,12},{12,16},{16,20},{20,24},{24,28},{28,0},{1,5},{5... | collective-permute-start | bytes 1179656 | tf_op jit(solution)/shard_map/ppermute | solution.py:37
  13.0 7.0 %collective-permute-start.1 = (bf16[384,256]{1,0:T(8,128)(2,1)S(1)}, bf16[384,256]{1,0:T(8,128)(2,1)S(1)}, u32[]{:S(2)}, u32[]{:S(2)}) collective-permute-start(bf16[384,256]{1,0:T(8,128)(2,1)S(1)} %collective-permute-done.refs_2_), channel_id=1, source_target_pairs={{0,2},{1,3},{2,0},{3,1},{4,6},{5,7},{6,4},{7,5},{8,10},{9,11},{10,... | collective-permute-start | bytes 589832 | tf_op jit(solution)/shard_map/ppermute | solution.py:47
  14.5 6.7 %collective-permute-start.3 = (bf16[384,256]{1,0:T(8,128)(2,1)S(1)}, bf16[384,256]{1,0:T(8,128)(2,1)S(1)}, u32[]{:S(2)}, u32[]{:S(2)}) collective-permute-start(bf16[384,256]{1,0:T(8,128)(2,1)S(1)} %collective-permute-done.2.refs_5_), channel_id=1, source_target_pairs={{0,1},{1,0},{2,3},{3,2},{4,5},{5,4},{6,7},{7,6},{8,9},{9,8},{10,11... | collective-permute-start | bytes 589832 | tf_op jit(solution)/shard_map/ppermute | solution.py:47
  21.3 32.2 %collective-permute-start.6 = (bf16[128,4096]{1,0:T(8,128)(2,1)S(1)}, bf16[128,4096]{1,0:T(8,128)(2,1)S(1)}, u32[]{:S(2)}, u32[]{:S(2)}) collective-permute-start(bf16[128,4096]{1,0:T(8,128)(2,1)S(1)} %shard_map.58), channel_id=1, source_target_pairs={{0,4},{4,8},{8,12},{12,16},{16,20},{20,24},{24,28},{28,0},{1,5},{5... | collective-permute-start | bytes 3145736 | tf_op jit(solution)/shard_map/ppermute | solution.py:37
  25.8 27.6 %collective-permute-start.7 = (bf16[128,4096]{1,0:T(8,128)(2,1)S(1)}, bf16[128,4096]{1,0:T(8,128)(2,1)S(1)}, u32[]{:S(2)}, u32[]{:S(2)}) collective-permute-start(bf16[128,4096]{1,0:T(8,128)(2,1)S(1)} %shard_map.59), channel_id=1, source_target_pairs={{0,4},{4,0},{8,12},{12,8},{16,20},{20,16},{24,28},{28,24},{1,5},{5... | collective-permute-start | bytes 3145736 | tf_op jit(solution)/shard_map/ppermute | solution.py:42
  29.4 6.1 %collective-permute-start.10 = (bf16[384,256]{1,0:T(8,128)(2,1)S(1)}, bf16[384,256]{1,0:T(8,128)(2,1)S(1)}, u32[]{:S(2)}, u32[]{:S(2)}) collective-permute-start(bf16[384,256]{1,0:T(8,128)(2,1)S(1)} %get-tuple-element.30), channel_id=1, source_target_pairs={{0,1},{1,0},{2,3},{3,2},{4,5},{5,4},{6,7},{7,6},{8,9},{9,8},{10,11... | collective-permute-start | bytes 589832 | tf_op jit(solution)/shard_map/ppermute | solution.py:47
  31.4 6.8 %collective-permute-start.12 = (bf16[384,256]{1,0:T(8,128)(2,1)S(1)}, bf16[384,256]{1,0:T(8,128)(2,1)S(1)}, u32[]{:S(2)}, u32[]{:S(2)}) collective-permute-start(bf16[384,256]{1,0:T(8,128)(2,1)S(1)} %get-tuple-element.29), channel_id=1, source_target_pairs={{0,2},{1,3},{2,0},{3,1},{4,6},{5,7},{6,4},{7,5},{8,10},{9,11},{10,... | collective-permute-start | bytes 589832 | tf_op jit(solution)/shard_map/ppermute | solution.py:47
  35.5 6.0 %collective-permute-start.14 = (bf16[384,256]{1,0:T(8,128)(2,1)S(1)}, bf16[384,256]{1,0:T(8,128)(2,1)S(1)}, u32[]{:S(2)}, u32[]{:S(2)}) collective-permute-start(bf16[384,256]{1,0:T(8,128)(2,1)S(1)} %get-tuple-element.29), channel_id=1, source_target_pairs={{0,1},{1,0},{2,3},{3,2},{4,5},{5,4},{6,7},{7,6},{8,9},{9,8},{10,11... | collective-permute-start | bytes 589832 | tf_op jit(solution)/shard_map/ppermute | solution.py:47
  38.2 6.2 %collective-permute-start.15 = (bf16[384,256]{1,0:T(8,128)(2,1)S(1)}, bf16[384,256]{1,0:T(8,128)(2,1)S(1)}, u32[]{:S(2)}, u32[]{:S(2)}) collective-permute-start(bf16[384,256]{1,0:T(8,128)(2,1)S(1)} %get-tuple-element.30), channel_id=1, source_target_pairs={{0,2},{1,3},{2,0},{3,1},{4,6},{5,7},{6,4},{7,5},{8,10},{9,11},{10,... | collective-permute-start | bytes 589832 | tf_op jit(solution)/shard_map/ppermute | solution.py:47
  41.6 7.1 %collective-permute-start.11 = (bf16[384,256]{1,0:T(8,128)(2,1)S(1)}, bf16[384,256]{1,0:T(8,128)(2,1)S(1)}, u32[]{:S(2)}, u32[]{:S(2)}) collective-permute-start(bf16[384,256]{1,0:T(8,128)(2,1)S(1)} %collective-permute-done.10.refs_2_), channel_id=1, source_target_pairs={{0,2},{1,3},{2,0},{3,1},{4,6},{5,7},{6,4},{7,5},{8,10},{9,11},{10,... | collective-permute-start | bytes 589832 | tf_op jit(solution)/shard_map/ppermute | solution.py:47
  44.4 5.7 %collective-permute-start.13 = (bf16[384,256]{1,0:T(8,128)(2,1)S(1)}, bf16[384,256]{1,0:T(8,128)(2,1)S(1)}, u32[]{:S(2)}, u32[]{:S(2)}) collective-permute-start(bf16[384,256]{1,0:T(8,128)(2,1)S(1)} %collective-permute-done.12.refs_5_), channel_id=1, source_target_pairs={{0,1},{1,0},{2,3},{3,2},{4,5},{5,4},{6,7},{7,6},{8,9},{9,8},{10,11... | collective-permute-start | bytes 589832 | tf_op jit(solution)/shard_map/ppermute | solution.py:47

commit v4 on v3

--- a/solution.py
+++ b/solution.py
@@ -147,6 +147,13 @@
     return place < length
 
 
+def causal_mask(rows):
+    causal = lax.broadcasted_iota(jnp.int32, (rows, rows), 1) <= lax.broadcasted_iota(
+        jnp.int32, (rows, rows), 0
+    )
+    return jnp.concatenate([causal] * STEP_HEADS, axis=0)
+
+
 def run_on_side(body, side, *refs):
     if side is None:
         body(*refs)
@@ -159,11 +166,15 @@
     return keys, jnp.concatenate([part[:, HEAD_SIZE:] for part in parts], axis=0)
 
 
-def near_kernel(rows, side, *refs):
-    run_on_side(functools.partial(near_body, rows), side, *refs)
-
-
-def near_body(rows, query, own, *rest):
+def near_kernel(rows, own_sides, *refs):
+    if len(own_sides) == 2:
+        near_body(rows, True, *refs)
+    else:
+        for side in (0, 1):
+            run_on_side(functools.partial(near_body, rows, side in own_sides), side, *refs)
+
+
+def near_body(rows, with_own, query, own, *rest):
     halves, (top_ref, sums_ref, beside, above) = rest[:4], rest[4:]
     me = lax.axis_index("sp")
     heads = own_heads(query, rows)
@@ -176,10 +187,12 @@
     blocks = (own, beside, above)
     live = live_mask(query, positions)
     step_rows = STEP_HEADS * rows
+    causal = causal_mask(rows)
     for offset in range(len(blocks) + 1):
         head = me ^ offset
         start = pl.multiple_of(head * rows + jnp.where(head >= heads // 2, positions, 0), rows)
-        parts = [block[pl.ds(start, rows), :] for block in blocks[1:]]
+        near_blocks = blocks if with_own else blocks[1:]
+        parts = [block[pl.ds(start, rows), :] for block in near_blocks]
         if offset < len(blocks):
             parts.append(blocks[offset][middle : middle + positions, :])
         keys, values = stored_parts(parts)
@@ -188,11 +201,14 @@
             place = pl.ds(base + step * step_rows, step_rows)
             scores = dot_scores(query[place, :], keys)
             pieces = []
+            if with_own:
+                pieces.append(jnp.where(causal, scores[:, :rows], MASKED))
             for other in range(1, len(blocks)):
-                piece = scores[:, (other - 1) * rows : other * rows]
+                left = len(pieces) * rows
+                piece = scores[:, left : left + rows]
                 pieces.append(jnp.where((me ^ other) < me, piece, MASKED))
             if offset < len(blocks):
-                pieces.append(jnp.where(live, scores[:, (len(blocks) - 1) * rows :], MASKED))
+                pieces.append(jnp.where(live, scores[:, len(pieces) * rows :], MASKED))
             scores = jnp.concatenate(pieces, axis=1)
             top = jnp.max(scores, axis=1, keepdims=True)
             weights = jnp.exp2((scores - top) * FACTOR).astype(jnp.bfloat16)
@@ -200,11 +216,11 @@
             top_ref[place, :] = jnp.broadcast_to(top, (step_rows, HEAD_SIZE))
 
 
-def far_kernel(rows, stride, side, *refs):
-    run_on_side(functools.partial(far_body, rows, stride), side, *refs)
-
-
-def far_body(rows, stride, query, own, first_half, second_half, top_ref, sums_ref, *rest):
+def far_kernel(rows, stride, with_own, side, *refs):
+    run_on_side(functools.partial(far_body, rows, stride, with_own), side, *refs)
+
+
+def far_body(rows, stride, with_own, query, own, first_half, second_half, top_ref, sums_ref, *rest):
     out, across, results, sem = rest if len(rest) == 4 else (*rest, None, None)
     me = lax.axis_index("sp")
     heads = own_heads(query, rows)
@@ -216,16 +232,14 @@
     across[half:, :] = second_half[...]
     live = live_mask(query, positions)
     step_rows = STEP_HEADS * rows
-    causal = lax.broadcasted_iota(jnp.int32, (rows, rows), 1) <= lax.broadcasted_iota(
-        jnp.int32, (rows, rows), 0
-    )
-    causal = jnp.concatenate([causal] * STEP_HEADS, axis=0)
+    causal = causal_mask(rows)
     far = heads - 1
     copies = []
     for offset in range(heads):
         head = me ^ offset
         start = pl.multiple_of(head * rows + jnp.where(head >= heads // 2, positions, 0), rows)
-        parts = [own[pl.ds(start, rows), :], across[pl.ds(start, rows), :]]
+        far_blocks = (own, across) if with_own else (across,)
+        parts = [block[pl.ds(start, rows), :] for block in far_blocks]
         if offset == far:
             parts.append(across[middle : middle + positions, :])
         keys, values = stored_parts(parts)
@@ -233,12 +247,13 @@
         for step in range(GROUP // STEP_HEADS):
             place = pl.ds(base + step * step_rows, step_rows)
             scores = dot_scores(query[place, :], keys)
-            pieces = [
-                jnp.where(causal, scores[:, :rows], MASKED),
-                jnp.where((me ^ far) < me, scores[:, rows : 2 * rows], MASKED),
-            ]
+            pieces = []
+            if with_own:
+                pieces.append(jnp.where(causal, scores[:, :rows], MASKED))
+            left = len(pieces) * rows
+            pieces.append(jnp.where((me ^ far) < me, scores[:, left : left + rows], MASKED))
             if offset == far:
-                pieces.append(jnp.where(live, scores[:, 2 * rows :], MASKED))
+                pieces.append(jnp.where(live, scores[:, left + rows :], MASKED))
             scores = jnp.concatenate(pieces, axis=1)
             before = top_ref[place, :]
             top = jnp.maximum(jnp.max(scores, axis=1, keepdims=True), before)
@@ -290,11 +305,11 @@
         run_on_side(place, side, passed)
 
 
-def near(turned, rows, own, beside, above, side=None):
+def near(turned, rows, own, beside, above, own_sides):
     block = pltpu.VMEM(own.shape, jnp.bfloat16)
     work = turned.shape[0] * 5 * rows
     return pl.pallas_call(
-        functools.partial(near_kernel, rows, side),
+        functools.partial(near_kernel, rows, own_sides),
         out_shape=[
             pltpu.VMEM((turned.shape[0] - LENGTH_ROWS, HEAD_SIZE), jnp.float32),
             pltpu.VMEM((turned.shape[0] - LENGTH_ROWS, 2 * HEAD_SIZE), jnp.float32),
@@ -309,7 +324,7 @@
     )(turned, own, *beside, *above)
 
 
-def far(turned, rows, own, first_half, second_half, state, stride=1, side=None):
+def far(turned, rows, own, first_half, second_half, state, with_own, stride=1, side=None):
     work = turned.shape[0] * 2 * rows
     width = (turned.shape[0] - LENGTH_ROWS) // rows * HEAD_SIZE
     heads = width // (GROUP * HEAD_SIZE)
@@ -319,7 +334,7 @@
         scratch.append(pltpu.SemaphoreType.DMA((heads,)))
     place = pltpu.VMEM if stride == 1 else pltpu.HBM
     return pl.pallas_call(
-        functools.partial(far_kernel, rows, stride, side),
+        functools.partial(far_kernel, rows, stride, with_own, side),
         out_shape=place((rows, width * stride), jnp.bfloat16),
         in_specs=[VMEM] * 6,
         out_specs=pl.BlockSpec(memory_space=place),
@@ -479,15 +494,15 @@
     moved_above = [partner_swap(moved_pack[half:], 2)]
     moved_beside.append(partner_swap(moved_pack[half:], 1))
     moved_above.insert(0, partner_swap(moved_pack[:half], 2))
-    state = near(turned_here, rows, here, beside, above)
-    attended = far(turned_here, rows, here, first_half, second_half, state, side=1)
+    state = near(turned_here, rows, here, beside, above, (1,))
+    attended = far(turned_here, rows, here, first_half, second_half, state, False, side=1)
     from_odd = section_shift(attended)
-    attended = far(turned_here, rows, here, first_half, second_half, state, side=0)
+    attended = far(turned_here, rows, here, first_half, second_half, state, True, side=0)
     from_even = section_swap(attended)
     moved_first = partner_swap(moved_beside[0], 2)
     moved_second = partner_swap(moved_above[1], 1)
-    state = near(moved_query, rows, moved_pack, moved_beside, moved_above)
-    out = far(moved_query, rows, moved_pack, moved_first, moved_second, state, chunks)
+    state = near(moved_query, rows, moved_pack, moved_beside, moved_above, (0, 1))
+    out = far(moved_query, rows, moved_pack, moved_first, moved_second, state, False, chunks)
     out = pl.pallas_call(
         join_kernel,
         out_shape=pltpu.HBM(out.shape, out.dtype),

time: 54.8 us -> 54.3 us (level)
  waiting for transfers between devices: 16.6 us -> 16 us
  Pallas kernels: 14.4 us -> 15 us
    ppermute x12, waiting for transfers between devices: 13.1 us -> 11.8 us  [partner_swap(): return lax.ppermute(value, 'sp', [(i, i ^ bits) for i in range(count)])]
    ppermute x3, waiting for transfers between devices: 3.5 us -> 4.21 us  [section_shift(): lax.ppermute(value, 'section', [(i, (i + 1) % count) for i in range(count)])]
    pallas_call x5, Pallas kernels: 10.9 us -> 11.5 us  [the longest x2 6.09 us: near(): pl.pallas_call(functools.partial(near_kernel, rows, own_sides), out_shape...]
  transfers between devices with their start and end apart: 16 -> 16, of which waited for: 10 -> 10; matrix products, arithmetic and copies ran while one was open for 0% -> 0% of each run, Pallas kernels for 22% -> 23%
where the time goes in v4:
time: 54.3 us; the launch traced here: 54.1 us
  starting transfers between devices  21.4 us (39%)
  waiting for transfers between devices  16 us (29%)
  Pallas kernels  15 us (28%)
  between operations  1.59 us (3%)
    ppermute x12, starting transfers between devices, partner_swap(): return lax.ppermute(value, 'sp', [(i, i ^ bits) for i in range(count)])  19.8 us
    ppermute x12, waiting for transfers between devices, partner_swap(): return lax.ppermute(value, 'sp', [(i, i ^ bits) for i in range(count)])  11.8 us
    pallas_call x2, Pallas kernels, near(): pl.pallas_call(functools.partial(near_kernel, rows, own_sides), out_shape...  6.09 us
    pallas_call x3, Pallas kernels, far(): pl.pallas_call(functools.partial(far_kernel, rows, stride, with_own, side...  5.44 us
    ppermute x3, waiting for transfers between devices, section_shift(): lax.ppermute(value, 'section', [(i, (i + 1) % count) for i in range(count)])  4.21 us
    ppermute x3, starting transfers between devices, section_shift(): lax.ppermute(value, 'section', [(i, (i + 1) % count) for i in range(count)])  1.53 us
    pallas_call x1, Pallas kernels, on_device(): pl.pallas_call(pack_kernel, out_shape=[pack] * chunks + [table] * 2, in_s...  1.42 us
  transfers between devices with their start and end apart: 16, of which 10 were waited for; matrix products, arithmetic and copies ran while one was open for 0% of the time, Pallas kernels for 23%

profile of v4, /device:TPU:0, one launch (start us, length us, event | category | flops | bytes accessed | tf_op | source)
XLA Modules:
  0.0 54.1 jit_solution(15570836548278897940)
XLA Ops:
  0.0 0.1 maximum_bitcast_fusion.frequency
  0.7 0.0 copy-start
  0.8 1.4 %shard_map.55 = (bf16[768,256]{1,0:T(8,128)(2,1)S(1)}, bf16[768,256]{1,0:T(8,128)(2,1)S(1)}, f32[128,128]{1,0:T(8,128)S(1)}, f32[128,128]{1,0:T(8,128)S(1)}) custom-call(bf16[128,2048]{1,0:T(8,128)(2,1)} %bitcast.7, bf16[2,256,256]{2,1,0:T(8,128)(2,1)} %bitcast.8, f32[1,128]{1,0:T(1,128)S(1)} %maximum_bitcast_fusion.frequency, s32[1]{0:T(128)S(6)} %copy.8.offset), custom_call_target="tpu_custom_call" | custom-call | flops 1073741824 | bytes 2097152 | tf_op jit(solution)/shard_map/pallas_call | solution.py:462
  2.2 3.0 %collective-permute-start = (bf16[384,256]{1,0:T(8,128)(2,1)S(1)}, bf16[384,256]{1,0:T(8,128)(2,1)S(1)}, u32[]{:S(2)}, u32[]{:S(2)}) collective-permute-start(bf16[384,256]{1,0:T(8,128)(2,1)S(1)} %get-tuple-element.32), channel_id=1, source_target_pairs={{0,1},{1,0},{2,3},{3,2},{4,5},{5,4},{6,7},{7,6},{8,9},{9,8},{10,11... | collective-permute-start | bytes 589832 | tf_op jit(solution)/shard_map/ppermute | solution.py:47
  5.3 1.5 %collective-permute-start.2 = (bf16[384,256]{1,0:T(8,128)(2,1)S(1)}, bf16[384,256]{1,0:T(8,128)(2,1)S(1)}, u32[]{:S(2)}, u32[]{:S(2)}) collective-permute-start(bf16[384,256]{1,0:T(8,128)(2,1)S(1)} %get-tuple-element.31), channel_id=1, source_target_pairs={{0,2},{1,3},{2,0},{3,1},{4,6},{5,7},{6,4},{7,5},{8,10},{9,11},{10,... | collective-permute-start | bytes 589832 | tf_op jit(solution)/shard_map/ppermute | solution.py:47
  6.8 0.5 collective-permute-start.4
  7.3 0.1 collective-permute-start.5
  8.0 0.0 copy-done
  8.0 1.0 %shard_map.56 = (bf16[4112,128]{1,0:T(8,128)(2,1)S(1)}, bf16[4112,128]{1,0:T(8,128)(2,1)S(1)}) custom-call(bf16[128,8192]{1,0:T(8,128)(2,1)S(1)} %bitcast.6, f32[128,128]{1,0:T(8,128)S(1)} %get-tuple-element.18.cosine, f32[128,128]{1,0:T(8,128)S(1)} %get-tuple-element.19.sine, s32[1]{0:T(128)S(6)} %copy.9.length), custom_call_target="tpu_custom_call" | custom-call | flops 1073741824 | bytes 8388608 | tf_op jit(solution)/shard_map/pallas_call | solution.py:477
  9.1 0.1 collective-permute-start.8
  9.1 1.9 %collective-permute-done.refs_2_ = bf16[384,256]{1,0:T(8,128)(2,1)S(1)} collective-permute-done((bf16[384,256]{1,0:T(8,128)(2,1)S(1)}, bf16[384,256]{1,0:T(8,128)(2,1)S(1)}, u32[]{:S(2)}, u32[]{:S(2)}) %collective-permute-start) | collective-permute-done | bytes 196640 | tf_op jit(solution)/shard_map/ppermute | solution.py:47
  11.0 0.3 collective-permute-start.9
  11.3 1.8 %collective-permute-done.2.refs_5_ = bf16[384,256]{1,0:T(8,128)(2,1)S(1)} collective-permute-done((bf16[384,256]{1,0:T(8,128)(2,1)S(1)}, bf16[384,256]{1,0:T(8,128)(2,1)S(1)}, u32[]{:S(2)}, u32[]{:S(2)}) %collective-permute-start.2) | collective-permute-done | bytes 196640 | tf_op jit(solution)/shard_map/ppermute | solution.py:47
  13.0 1.5 %collective-permute-start.1 = (bf16[384,256]{1,0:T(8,128)(2,1)S(1)}, bf16[384,256]{1,0:T(8,128)(2,1)S(1)}, u32[]{:S(2)}, u32[]{:S(2)}) collective-permute-start(bf16[384,256]{1,0:T(8,128)(2,1)S(1)} %collective-permute-done.refs_2_), channel_id=1, source_target_pairs={{0,2},{1,3},{2,0},{3,1},{4,6},{5,7},{6,4},{7,5},{8,10},{9,11},{10,... | collective-permute-start | bytes 589832 | tf_op jit(solution)/shard_map/ppermute | solution.py:47
  14.5 0.0 collective-permute-done.4.refs_3_
  14.5 1.6 %collective-permute-start.3 = (bf16[384,256]{1,0:T(8,128)(2,1)S(1)}, bf16[384,256]{1,0:T(8,128)(2,1)S(1)}, u32[]{:S(2)}, u32[]{:S(2)}) collective-permute-start(bf16[384,256]{1,0:T(8,128)(2,1)S(1)} %collective-permute-done.2.refs_5_), channel_id=1, source_target_pairs={{0,1},{1,0},{2,3},{3,2},{4,5},{5,4},{6,7},{7,6},{8,9},{9,8},{10,11... | collective-permute-start | bytes 589832 | tf_op jit(solution)/shard_map/ppermute | solution.py:47
  16.1 0.0 collective-permute-done.5.refs_4_
  16.1 2.4 %shard_map.57 = (f32[4096,128]{1,0:T(8,128)S(1)}, f32[4096,256]{1,0:T(8,128)S(1)}) custom-call(bf16[4112,128]{1,0:T(8,128)(2,1)S(1)} %get-tuple-element.21.refs_0_, bf16[768,256]{1,0:T(8,128)(2,1)S(1)} %get-tuple-element.22.refs_1_, bf16[384,256]{1,0:T(8,128)(2,1)S(1)} %collective-permute-done.refs_2_, bf16[384,256]{1,0:T(8,128)(2,1)S(1)} %collective-permute-done.4.refs_3_, ...), custom_call_target="tpu_custom_call" | custom-call | flops 4042260480 | bytes 2105344 | tf_op jit(solution)/shard_map/pallas_call | solution.py:311
  18.5 1.5 %collective-permute-done.1.refs_2_ = bf16[384,256]{1,0:T(8,128)(2,1)S(1)} collective-permute-done((bf16[384,256]{1,0:T(8,128)(2,1)S(1)}, bf16[384,256]{1,0:T(8,128)(2,1)S(1)}, u32[]{:S(2)}, u32[]{:S(2)}) %collective-permute-start.1) | collective-permute-done | bytes 196640 | tf_op jit(solution)/shard_map/ppermute | solution.py:47
  20.0 1.2 %collective-permute-done.3.refs_3_ = bf16[384,256]{1,0:T(8,128)(2,1)S(1)} collective-permute-done((bf16[384,256]{1,0:T(8,128)(2,1)S(1)}, bf16[384,256]{1,0:T(8,128)(2,1)S(1)}, u32[]{:S(2)}, u32[]{:S(2)}) %collective-permute-start.3) | collective-permute-done | bytes 196640 | tf_op jit(solution)/shard_map/ppermute | solution.py:47
  21.3 1.2 %collective-permute-start.6 = (bf16[128,4096]{1,0:T(8,128)(2,1)S(1)}, bf16[128,4096]{1,0:T(8,128)(2,1)S(1)}, u32[]{:S(2)}, u32[]{:S(2)}) collective-permute-start(bf16[128,4096]{1,0:T(8,128)(2,1)S(1)} %shard_map.58), channel_id=1, source_target_pairs={{0,4},{4,8},{8,12},{12,16},{16,20},{20,24},{24,28},{28,0},{1,5},{5... | collective-permute-start | bytes 3145736 | tf_op jit(solution)/shard_map/ppermute | solution.py:37
  22.5 2.6 %shard_map.59 = bf16[128,4096]{1,0:T(8,128)(2,1)S(1)} custom-call(bf16[4112,128]{1,0:T(8,128)(2,1)S(1)} %get-tuple-element.21.refs_0_, bf16[768,256]{1,0:T(8,128)(2,1)S(1)} %get-tuple-element.22.refs_1_, bf16[384,256]{1,0:T(8,128)(2,1)S(1)} %collective-permute-done.1.refs_2_, bf16[384,256]{1,0:T(8,128)(2,1)S(1)} %collective-permute-done.3.refs_3_, ...), custom_call_target="tpu_custom_call" | custom-call | flops 1616904192 | bytes 2105344 | tf_op jit(solution)/shard_map/pallas_call | solution.py:336
  25.1 0.1 collective-permute-start.7
  25.2 4.2 %collective-permute-done.9.refs_1_ = bf16[768,256]{1,0:T(8,128)(2,1)S(1)} collective-permute-done((bf16[768,256]{1,0:T(8,128)(2,1)S(1)}, bf16[768,256]{1,0:T(8,128)(2,1)S(1)}, u32[]{:S(2)}, u32[]{:S(2)}) %collective-permute-start.9) | collective-permute-done | bytes 393248 | tf_op jit(solution)/shard_map/ppermute | solution.py:37
  29.4 2.0 %collective-permute-start.10 = (bf16[384,256]{1,0:T(8,128)(2,1)S(1)}, bf16[384,256]{1,0:T(8,128)(2,1)S(1)}, u32[]{:S(2)}, u32[]{:S(2)}) collective-permute-start(bf16[384,256]{1,0:T(8,128)(2,1)S(1)} %get-tuple-element.30), channel_id=1, source_target_pairs={{0,1},{1,0},{2,3},{3,2},{4,5},{5,4},{6,7},{7,6},{8,9},{9,8},{10,11... | collective-permute-start | bytes 589832 | tf_op jit(solution)/shard_map/ppermute | solution.py:47
  31.4 1.5 %collective-permute-start.12 = (bf16[384,256]{1,0:T(8,128)(2,1)S(1)}, bf16[384,256]{1,0:T(8,128)(2,1)S(1)}, u32[]{:S(2)}, u32[]{:S(2)}) collective-permute-start(bf16[384,256]{1,0:T(8,128)(2,1)S(1)} %get-tuple-element.29), channel_id=1, source_target_pairs={{0,2},{1,3},{2,0},{3,1},{4,6},{5,7},{6,4},{7,5},{8,10},{9,11},{10,... | collective-permute-start | bytes 589832 | tf_op jit(solution)/shard_map/ppermute | solution.py:47
  33.0 2.6 %collective-permute-done.10.refs_2_ = bf16[384,256]{1,0:T(8,128)(2,1)S(1)} collective-permute-done((bf16[384,256]{1,0:T(8,128)(2,1)S(1)}, bf16[384,256]{1,0:T(8,128)(2,1)S(1)}, u32[]{:S(2)}, u32[]{:S(2)}) %collective-permute-start.10) | collective-permute-done | bytes 196640 | tf_op jit(solution)/shard_map/ppermute | solution.py:47
  35.5 2.4 %collective-permute-start.14 = (bf16[384,256]{1,0:T(8,128)(2,1)S(1)}, bf16[384,256]{1,0:T(8,128)(2,1)S(1)}, u32[]{:S(2)}, u32[]{:S(2)}) collective-permute-start(bf16[384,256]{1,0:T(8,128)(2,1)S(1)} %get-tuple-element.29), channel_id=1, source_target_pairs={{0,1},{1,0},{2,3},{3,2},{4,5},{5,4},{6,7},{7,6},{8,9},{9,8},{10,11... | collective-permute-start | bytes 589832 | tf_op jit(solution)/shard_map/ppermute | solution.py:47
  38.0 0.3 collective-permute-done.12.refs_5_
  38.2 1.5 %collective-permute-start.15 = (bf16[384,256]{1,0:T(8,128)(2,1)S(1)}, bf16[384,256]{1,0:T(8,128)(2,1)S(1)}, u32[]{:S(2)}, u32[]{:S(2)}) collective-permute-start(bf16[384,256]{1,0:T(8,128)(2,1)S(1)} %get-tuple-element.30), channel_id=1, source_target_pairs={{0,2},{1,3},{2,0},{3,1},{4,6},{5,7},{6,4},{7,5},{8,10},{9,11},{10,... | collective-permute-start | bytes 589832 | tf_op jit(solution)/shard_map/ppermute | solution.py:47
  39.7 1.9 %collective-permute-done.14.refs_3_ = bf16[384,256]{1,0:T(8,128)(2,1)S(1)} collective-permute-done((bf16[384,256]{1,0:T(8,128)(2,1)S(1)}, bf16[384,256]{1,0:T(8,128)(2,1)S(1)}, u32[]{:S(2)}, u32[]{:S(2)}) %collective-permute-start.14) | collective-permute-done | bytes 196640 | tf_op jit(solution)/shard_map/ppermute | solution.py:47
  41.6 2.3 %collective-permute-start.11 = (bf16[384,256]{1,0:T(8,128)(2,1)S(1)}, bf16[384,256]{1,0:T(8,128)(2,1)S(1)}, u32[]{:S(2)}, u32[]{:S(2)}) collective-permute-start(bf16[384,256]{1,0:T(8,128)(2,1)S(1)} %collective-permute-done.10.refs_2_), channel_id=1, source_target_pairs={{0,2},{1,3},{2,0},{3,1},{4,6},{5,7},{6,4},{7,5},{8,10},{9,11},{10,... | collective-permute-start | bytes 589832 | tf_op jit(solution)/shard_map/ppermute | solution.py:47
  43.9 0.6 %collective-permute-done.15.refs_4_ = bf16[384,256]{1,0:T(8,128)(2,1)S(1)} collective-permute-done((bf16[384,256]{1,0:T(8,128)(2,1)S(1)}, bf16[384,256]{1,0:T(8,128)(2,1)S(1)}, u32[]{:S(2)}, u32[]{:S(2)}) %collective-permute-start.15) | collective-permute-done | bytes 196640 | tf_op jit(solution)/shard_map/ppermute | solution.py:47
  44.4 1.9 %collective-permute-start.13 = (bf16[384,256]{1,0:T(8,128)(2,1)S(1)}, bf16[384,256]{1,0:T(8,128)(2,1)S(1)}, u32[]{:S(2)}, u32[]{:S(2)}) collective-permute-start(bf16[384,256]{1,0:T(8,128)(2,1)S(1)} %collective-permute-done.12.refs_5_), channel_id=1, source_target_pairs={{0,1},{1,0},{2,3},{3,2},{4,5},{5,4},{6,7},{7,6},{8,9},{9,8},{10,11... | collective-permute-start | bytes 589832 | tf_op jit(solution)/shard_map/ppermute | solution.py:47
  46.3 0.0 collective-permute-done.8.refs_0_
  46.3 3.7 %shard_map.60 = (f32[4096,128]{1,0:T(8,128)S(1)}, f32[4096,256]{1,0:T(8,128)S(1)}) custom-call(bf16[4112,128]{1,0:T(8,128)(2,1)S(1)} %collective-permute-done.8.refs_0_, bf16[768,256]{1,0:T(8,128)(2,1)S(1)} %collective-permute-done.9.refs_1_, bf16[384,256]{1,0:T(8,128)(2,1)S(1)} %collective-permute-done.10.refs_2_, ...), custom_call_target="tpu_custom_call" | custom-call | flops 4042260480 | bytes 2105344 | tf_op jit(solution)/shard_map/pallas_call | solution.py:311
  50.0 0.0 collective-permute-done.11.refs_2_
  50.0 0.1 collective-permute-done.13.refs_3_
  50.1 2.8 %shard_map.61.before = bf16[128,8192]{1,0:T(8,128)(2,1)} custom-call(bf16[4112,128]{1,0:T(8,128)(2,1)S(1)} %collective-permute-done.8.refs_0_, bf16[768,256]{1,0:T(8,128)(2,1)S(1)} %collective-permute-done.9.refs_1_, bf16[384,256]{1,0:T(8,128)(2,1)S(1)} %collective-permute-done.11.refs_2_, bf16[384,256]{1,0:T(8,128)(2,1)S(1)} %collective-permute-done.13.refs_3_, ...), custom_call_target="tpu_custom_call" | custom-call | flops 1616904192 | bytes 2105344 | tf_op jit(solution)/shard_map/pallas_call | solution.py:336
  52.9 0.0 collective-permute-done.6.from_odd
  52.9 0.0 collective-permute-done.7.from_even
  52.9 1.0 %shard_map.62 = bf16[128,8192]{1,0:T(8,128)(2,1)} custom-call(bf16[128,4096]{1,0:T(8,128)(2,1)S(1)} %collective-permute-done.6.from_odd, bf16[128,4096]{1,0:T(8,128)(2,1)S(1)} %collective-permute-done.7.from_even, bf16[128,8192]{1,0:T(8,128)(2,1)} %shard_map.61.before), custom_call_target="tpu_custom_call", output_to_operand_aliasing={{}: (2, {})} | custom-call | flops 1048576 | bytes 2097152 | tf_op jit(solution)/shard_map/pallas_call | solution.py:506
  (4 shorter events, 0.1 us)
Async XLA Ops:
  0.7 7.3 %copy-start = (bf16[1,128,8192]{2,1,0:T(8,128)(2,1)S(1)}, bf16[1,128,8192]{2,1,0:T(8,128)(2,1)}, u32[]{:S(2)}) copy-start(bf16[1,128,8192]{2,1,0:T(8,128)(2,1)} %param.5) | copy-start | bytes 6291460
  2.2 8.8 %collective-permute-start = (bf16[384,256]{1,0:T(8,128)(2,1)S(1)}, bf16[384,256]{1,0:T(8,128)(2,1)S(1)}, u32[]{:S(2)}, u32[]{:S(2)}) collective-permute-start(bf16[384,256]{1,0:T(8,128)(2,1)S(1)} %get-tuple-element.32), channel_id=1, source_target_pairs={{0,1},{1,0},{2,3},{3,2},{4,5},{5,4},{6,7},{7,6},{8,9},{9,8},{10,11... | collective-permute-start | bytes 589832 | tf_op jit(solution)/shard_map/ppermute | solution.py:47
  5.3 7.8 %collective-permute-start.2 = (bf16[384,256]{1,0:T(8,128)(2,1)S(1)}, bf16[384,256]{1,0:T(8,128)(2,1)S(1)}, u32[]{:S(2)}, u32[]{:S(2)}) collective-permute-start(bf16[384,256]{1,0:T(8,128)(2,1)S(1)} %get-tuple-element.31), channel_id=1, source_target_pairs={{0,2},{1,3},{2,0},{3,1},{4,6},{5,7},{6,4},{7,5},{8,10},{9,11},{10,... | collective-permute-start | bytes 589832 | tf_op jit(solution)/shard_map/ppermute | solution.py:47
  6.8 7.8 %collective-permute-start.4 = (bf16[384,256]{1,0:T(8,128)(2,1)S(1)}, bf16[384,256]{1,0:T(8,128)(2,1)S(1)}, u32[]{:S(2)}, u32[]{:S(2)}) collective-permute-start(bf16[384,256]{1,0:T(8,128)(2,1)S(1)} %get-tuple-element.31), channel_id=1, source_target_pairs={{0,1},{1,0},{2,3},{3,2},{4,5},{5,4},{6,7},{7,6},{8,9},{9,8},{10,11... | collective-permute-start | bytes 589832 | tf_op jit(solution)/shard_map/ppermute | solution.py:47
  7.3 8.8 %collective-permute-start.5 = (bf16[384,256]{1,0:T(8,128)(2,1)S(1)}, bf16[384,256]{1,0:T(8,128)(2,1)S(1)}, u32[]{:S(2)}, u32[]{:S(2)}) collective-permute-start(bf16[384,256]{1,0:T(8,128)(2,1)S(1)} %get-tuple-element.32), channel_id=1, source_target_pairs={{0,2},{1,3},{2,0},{3,1},{4,6},{5,7},{6,4},{7,5},{8,10},{9,11},{10,... | collective-permute-start | bytes 589832 | tf_op jit(solution)/shard_map/ppermute | solution.py:47
  9.1 37.2 %collective-permute-start.8 = (bf16[4112,128]{1,0:T(8,128)(2,1)S(1)}, bf16[4112,128]{1,0:T(8,128)(2,1)S(1)}, u32[]{:S(2)}, u32[]{:S(2)}) collective-permute-start(bf16[4112,128]{1,0:T(8,128)(2,1)S(1)} %get-tuple-element.25), channel_id=1, source_target_pairs={{0,4},{4,8},{8,12},{12,16},{16,20},{20,24},{24,28},{28,0},{1,5},{5... | collective-permute-start | bytes 3158024 | tf_op jit(solution)/shard_map/ppermute | solution.py:37
  11.0 18.4 %collective-permute-start.9 = (bf16[768,256]{1,0:T(8,128)(2,1)S(1)}, bf16[768,256]{1,0:T(8,128)(2,1)S(1)}, u32[]{:S(2)}, u32[]{:S(2)}) collective-permute-start(bf16[768,256]{1,0:T(8,128)(2,1)S(1)} %get-tuple-element.26), channel_id=1, source_target_pairs={{0,4},{4,8},{8,12},{12,16},{16,20},{20,24},{24,28},{28,0},{1,5},{5... | collective-permute-start | bytes 1179656 | tf_op jit(solution)/shard_map/ppermute | solution.py:37
  13.0 7.0 %collective-permute-start.1 = (bf16[384,256]{1,0:T(8,128)(2,1)S(1)}, bf16[384,256]{1,0:T(8,128)(2,1)S(1)}, u32[]{:S(2)}, u32[]{:S(2)}) collective-permute-start(bf16[384,256]{1,0:T(8,128)(2,1)S(1)} %collective-permute-done.refs_2_), channel_id=1, source_target_pairs={{0,2},{1,3},{2,0},{3,1},{4,6},{5,7},{6,4},{7,5},{8,10},{9,11},{10,... | collective-permute-start | bytes 589832 | tf_op jit(solution)/shard_map/ppermute | solution.py:47
  14.5 6.7 %collective-permute-start.3 = (bf16[384,256]{1,0:T(8,128)(2,1)S(1)}, bf16[384,256]{1,0:T(8,128)(2,1)S(1)}, u32[]{:S(2)}, u32[]{:S(2)}) collective-permute-start(bf16[384,256]{1,0:T(8,128)(2,1)S(1)} %collective-permute-done.2.refs_5_), channel_id=1, source_target_pairs={{0,1},{1,0},{2,3},{3,2},{4,5},{5,4},{6,7},{7,6},{8,9},{9,8},{10,11... | collective-permute-start | bytes 589832 | tf_op jit(solution)/shard_map/ppermute | solution.py:47
  21.3 31.6 %collective-permute-start.6 = (bf16[128,4096]{1,0:T(8,128)(2,1)S(1)}, bf16[128,4096]{1,0:T(8,128)(2,1)S(1)}, u32[]{:S(2)}, u32[]{:S(2)}) collective-permute-start(bf16[128,4096]{1,0:T(8,128)(2,1)S(1)} %shard_map.58), channel_id=1, source_target_pairs={{0,4},{4,8},{8,12},{12,16},{16,20},{20,24},{24,28},{28,0},{1,5},{5... | collective-permute-start | bytes 3145736 | tf_op jit(solution)/shard_map/ppermute | solution.py:37
  25.1 27.8 %collective-permute-start.7 = (bf16[128,4096]{1,0:T(8,128)(2,1)S(1)}, bf16[128,4096]{1,0:T(8,128)(2,1)S(1)}, u32[]{:S(2)}, u32[]{:S(2)}) collective-permute-start(bf16[128,4096]{1,0:T(8,128)(2,1)S(1)} %shard_map.59), channel_id=1, source_target_pairs={{0,4},{4,0},{8,12},{12,8},{16,20},{20,16},{24,28},{28,24},{1,5},{5... | collective-permute-start | bytes 3145736 | tf_op jit(solution)/shard_map/ppermute | solution.py:42
  29.4 6.1 %collective-permute-start.10 = (bf16[384,256]{1,0:T(8,128)(2,1)S(1)}, bf16[384,256]{1,0:T(8,128)(2,1)S(1)}, u32[]{:S(2)}, u32[]{:S(2)}) collective-permute-start(bf16[384,256]{1,0:T(8,128)(2,1)S(1)} %get-tuple-element.30), channel_id=1, source_target_pairs={{0,1},{1,0},{2,3},{3,2},{4,5},{5,4},{6,7},{7,6},{8,9},{9,8},{10,11... | collective-permute-start | bytes 589832 | tf_op jit(solution)/shard_map/ppermute | solution.py:47
  31.4 6.8 %collective-permute-start.12 = (bf16[384,256]{1,0:T(8,128)(2,1)S(1)}, bf16[384,256]{1,0:T(8,128)(2,1)S(1)}, u32[]{:S(2)}, u32[]{:S(2)}) collective-permute-start(bf16[384,256]{1,0:T(8,128)(2,1)S(1)} %get-tuple-element.29), channel_id=1, source_target_pairs={{0,2},{1,3},{2,0},{3,1},{4,6},{5,7},{6,4},{7,5},{8,10},{9,11},{10,... | collective-permute-start | bytes 589832 | tf_op jit(solution)/shard_map/ppermute | solution.py:47
  35.5 6.0 %collective-permute-start.14 = (bf16[384,256]{1,0:T(8,128)(2,1)S(1)}, bf16[384,256]{1,0:T(8,128)(2,1)S(1)}, u32[]{:S(2)}, u32[]{:S(2)}) collective-permute-start(bf16[384,256]{1,0:T(8,128)(2,1)S(1)} %get-tuple-element.29), channel_id=1, source_target_pairs={{0,1},{1,0},{2,3},{3,2},{4,5},{5,4},{6,7},{7,6},{8,9},{9,8},{10,11... | collective-permute-start | bytes 589832 | tf_op jit(solution)/shard_map/ppermute | solution.py:47
  38.2 6.2 %collective-permute-start.15 = (bf16[384,256]{1,0:T(8,128)(2,1)S(1)}, bf16[384,256]{1,0:T(8,128)(2,1)S(1)}, u32[]{:S(2)}, u32[]{:S(2)}) collective-permute-start(bf16[384,256]{1,0:T(8,128)(2,1)S(1)} %get-tuple-element.30), channel_id=1, source_target_pairs={{0,2},{1,3},{2,0},{3,1},{4,6},{5,7},{6,4},{7,5},{8,10},{9,11},{10,... | collective-permute-start | bytes 589832 | tf_op jit(solution)/shard_map/ppermute | solution.py:47
  41.6 8.4 %collective-permute-start.11 = (bf16[384,256]{1,0:T(8,128)(2,1)S(1)}, bf16[384,256]{1,0:T(8,128)(2,1)S(1)}, u32[]{:S(2)}, u32[]{:S(2)}) collective-permute-start(bf16[384,256]{1,0:T(8,128)(2,1)S(1)} %collective-permute-done.10.refs_2_), channel_id=1, source_target_pairs={{0,2},{1,3},{2,0},{3,1},{4,6},{5,7},{6,4},{7,5},{8,10},{9,11},{10,... | collective-permute-start | bytes 589832 | tf_op jit(solution)/shard_map/ppermute | solution.py:47
  44.4 5.7 %collective-permute-start.13 = (bf16[384,256]{1,0:T(8,128)(2,1)S(1)}, bf16[384,256]{1,0:T(8,128)(2,1)S(1)}, u32[]{:S(2)}, u32[]{:S(2)}) collective-permute-start(bf16[384,256]{1,0:T(8,128)(2,1)S(1)} %collective-permute-done.12.refs_5_), channel_id=1, source_target_pairs={{0,1},{1,0},{2,3},{3,2},{4,5},{5,4},{6,7},{7,6},{8,9},{9,8},{10,11... | collective-permute-start | bytes 589832 | tf_op jit(solution)/shard_map/ppermute | solution.py:47
